TPU v7x, 128 devices: a whole 4x4x4 slice. The times are simulated.
128 devices in a mesh: section: 8 (over y, core), tp: 16 (over x, z).
Axes of the slice: x: 4, y: 4, z: 4, core: 2. Of those that a mesh axis runs over, the one named last changes fastest.
Arguments:
- token_ids: int32 [2, 128], replicated, may hold values from 0 to 65535
- alpha_num: int32 [1], replicated, may hold values from 3 to 7
- embed_table: bfloat16 [65536, 8192], P('section', 'tp'), may hold values from -6 to 6
- norm_gain: float32 [8, 8192], P('section'), may hold values from 0.5 to 1.5
- w_query: bfloat16 [8, 8192, 4096], P('section', None, 'tp'), may hold values from -4 to 4
- w_key: bfloat16 [8, 8192, 512], P('section', None, 'tp'), may hold values from -4 to 4
- w_value: bfloat16 [8, 8192, 512], P('section', None, 'tp'), may hold values from -0.0625 to 0.0625
- w_out: bfloat16 [8, 4096, 8192], P('section', 'tp'), may hold values from -0.09375 to 0.09375
Outputs:
- layer_out: bfloat16 [8, 2, 128, 8192], P('section', None, 'tp')
- scales_in: float32 [8, 8192], P('section')
- scales_out: float32 [8, 4096], P('section', 'tp')
- smoothed_q: bfloat16 [8, 8192, 4096], P('section', None, 'tp')
- smoothed_k: bfloat16 [8, 8192, 512], P('section', None, 'tp')
- smoothed_v: bfloat16 [8, 8192, 512], P('section', None, 'tp')
All inputs are finite; a program needn't handle non-finite values.
Results may differ from a plain program's by a relative error of at most 0.028.
Values may be sent and summed in bfloat16 or wider, within the bound.
No kernel may reach another device: no remote copies, remote signals or barrier semaphores. Data moves between devices by JAX's collectives and lax.ppermute only.
A program may use at most 128 MiB of HBM per device.

v0:
```python
import math

import jax
import jax.numpy as jnp
from jax import lax
from jax.experimental import pallas as pl
from jax.experimental.pallas import tpu as pltpu
from jax.sharding import Mesh
from jax.sharding import PartitionSpec as P


HEAD_DIM = 128
TP = ("x", "zh", "zl")
HALF = ("x", "zh")
SECTION = ("y", "core")
N_Y = 4
N_CORE = 2
N_TP = 16
GAIN_ROWS = 16

norm_eps = 1e-05
stat_eps = 1e-05
rope_base = 500000.0


def copy_for_each(value, axis):
    count = lax.axis_size(axis)
    return lax.all_to_all(
        jnp.broadcast_to(value[None], (count, *value.shape)), axis, 0, 0, tiled=True
    )


def rope_tables(length, head_size):
    halves = head_size // 2
    freqs = jnp.exp(-math.log(rope_base) * 2.0 * jnp.arange(halves, dtype=jnp.float32) / head_size)
    angles = jnp.arange(length, dtype=jnp.float32)[:, None] * freqs[None, :]
    return (jnp.cos(angles), jnp.sin(angles))


def smoothing(act_peak, weight_peak, alpha_exp):
    return jnp.exp(
        alpha_exp * jnp.log(act_peak + stat_eps)
        - (1.0 - alpha_exp) * jnp.log(weight_peak + stat_eps)
    )


def fetch(choice, sources, target, sem):
    for number, source in enumerate(sources):

        @pl.when(choice == number)
        def _():
            pltpu.make_async_copy(source, target, sem).start()


def choice_of(state_ref):
    layer = state_ref[0]
    step = (state_ref[1] - layer // N_CORE + N_Y) % N_Y
    return jnp.where(layer % N_CORE == state_ref[2], step, step + N_Y)


def front_body(state_ref, x_ref, *refs):
    count = 2 * N_Y
    q_refs, kv_refs = refs[:count], refs[count : 2 * count]
    out_ref, q_buf, kv_buf, sems = refs[2 * count :]
    choice = choice_of(state_ref)
    fetch(choice, kv_refs, kv_buf, sems.at[0])
    fetch(choice, q_refs, q_buf, sems.at[1])
    values = x_ref[...].astype(jnp.float32)
    length, _ = values.shape
    square = jnp.sum(values * values, axis=1, keepdims=True)
    square = jnp.broadcast_to(square, (length, HEAD_DIM)).T[:8]
    high = square.astype(jnp.bfloat16)
    low = (square - high.astype(jnp.float32)).astype(jnp.bfloat16)
    pltpu.make_async_copy(kv_refs[0], kv_buf, sems.at[0]).wait()
    rows = kv_buf.shape[0] - GAIN_ROWS
    gain = kv_buf[rows:, :].astype(jnp.float32)
    gain = jnp.sum(gain, axis=0, keepdims=True)
    lhs = (values * gain).astype(jnp.bfloat16)
    kv_part = lax.dot_general(
        kv_buf[:rows, :], lhs, (((1,), (1,)), ((), ())), preferred_element_type=jnp.float32
    ).astype(jnp.bfloat16)
    pltpu.make_async_copy(q_refs[0], q_buf, sems.at[1]).wait()
    query = jnp.dot(lhs, q_buf[...], preferred_element_type=jnp.float32).astype(jnp.bfloat16)
    heads = query.shape[1] // HEAD_DIM
    for copy in range(N_Y):
        for h in range(heads):
            out_ref[copy, h * length : (h + 1) * length, :] = query[
                :, h * HEAD_DIM : (h + 1) * HEAD_DIM
            ]
        at = heads * length
        out_ref[copy, at : at + rows, :] = kv_part
        out_ref[copy, at + rows : at + rows + 8, :] = high
        out_ref[copy, at + rows + 8 :, :] = low


def back_body(
    state_ref, x_ref, sums_ref, kv_ref, cos_ref, sin_ref, cos_t_ref, sin_t_ref, *refs
):
    f32, bf16 = jnp.float32, jnp.bfloat16
    count = 2 * N_Y
    w_refs, g_refs = refs[:count], refs[count : 2 * count]
    out_ref, peaks_ref, w_buf, g_buf, sems = refs[2 * count :]
    choice = choice_of(state_ref)
    first_gain = g_refs[0].shape[0] - GAIN_ROWS
    g_refs = [ref.at[pl.ds(first_gain, GAIN_ROWS), :] for ref in g_refs]
    fetch(choice, g_refs, g_buf, sems.at[0])
    fetch(choice, w_refs, w_buf, sems.at[1])
    length, part = x_ref.shape
    query_cols = w_buf.shape[0]
    heads = query_cols // HEAD_DIM
    pieces = kv_ref.shape[0] // heads
    kv_cols = kv_ref.shape[1] // 2
    stat_at = heads * length + 2 * kv_cols
    square = sums_ref[stat_at : stat_at + 1, :] + sums_ref[stat_at + 8 : stat_at + 9, :]
    inverse = lax.rsqrt(square / (part * N_Y) + norm_eps)
    inverse = jnp.broadcast_to(inverse, (HEAD_DIM, length)).T
    rows = lax.broadcasted_iota(jnp.int32, (length, length), 0)
    cols = lax.broadcasted_iota(jnp.int32, (length, length), 1)
    halves = HEAD_DIM // 2
    outs = []
    for h in range(heads):
        of_head = [kv_ref[h * pieces + (piece ^ 1)] for piece in range(pieces)]
        key_t = jnp.concatenate([piece[:kv_cols] for piece in of_head], axis=0).astype(f32)
        value_t = jnp.concatenate([piece[kv_cols:] for piece in of_head], axis=0)
        turned = jnp.concatenate([key_t[halves:], key_t[:halves]], axis=0)
        key_rot = (key_t * cos_t_ref[...] + turned * sin_t_ref[...]).astype(bf16)
        query = sums_ref[h * length : (h + 1) * length, :] * inverse
        query_rot = query * cos_ref[...] + pltpu.roll(query, halves, 1) * sin_ref[...]
        scores = jnp.dot(query_rot.astype(bf16), key_rot, preferred_element_type=f32)
        scores = jnp.where(rows >= cols, scores / math.sqrt(HEAD_DIM), -1e30)
        scores = jnp.exp(scores - jnp.max(scores, axis=1, keepdims=True))
        probs = (scores / jnp.sum(scores, axis=1, keepdims=True)).astype(bf16)
        outs.append(
            lax.dot_general(
                probs, value_t, (((1,), (1,)), ((), ())), preferred_element_type=f32
            ).astype(bf16)
        )
    attended = jnp.concatenate(outs, axis=1)
    peaks_ref[:, part:] = jnp.max(jnp.abs(attended.astype(f32)), axis=0, keepdims=True)
    pltpu.make_async_copy(g_refs[0], g_buf, sems.at[0]).wait()
    for at in range(0, part, HEAD_DIM):
        block = x_ref[:, at : at + HEAD_DIM].astype(f32)
        gain = g_buf[:, at : at + HEAD_DIM].astype(f32)
        gain = jnp.sum(gain, axis=0, keepdims=True)
        normed = (block * inverse * gain).astype(bf16).astype(f32)
        peaks_ref[:, at : at + HEAD_DIM] = jnp.max(jnp.abs(normed), axis=0, keepdims=True)
    pltpu.make_async_copy(w_refs[0], w_buf, sems.at[1]).wait()
    out_ref[...] = jnp.dot(attended, w_buf[...], preferred_element_type=f32).astype(bf16)


def front(state, gathered, blocks_q, blocks_kv):
    length = gathered.shape[0]
    rows = blocks_q[0].shape[1] + blocks_kv[0].shape[0]
    hbm = pl.BlockSpec(memory_space=pl.ANY)
    vmem = pl.BlockSpec(memory_space=pltpu.VMEM)
    return pl.pallas_call(
        front_body,
        out_shape=jax.ShapeDtypeStruct((N_Y, rows, length), jnp.bfloat16),
        in_specs=[pl.BlockSpec(memory_space=pltpu.SMEM), vmem, *[hbm] * (4 * N_Y)],
        out_specs=vmem,
        scratch_shapes=[
            pltpu.VMEM(blocks_q[0].shape, jnp.bfloat16),
            pltpu.VMEM(blocks_kv[0].shape, jnp.bfloat16),
            pltpu.SemaphoreType.DMA((2,)),
        ],
        compiler_params=pltpu.CompilerParams(vmem_limit_bytes=16 << 20),
        name="front",
    )(state, gathered, *blocks_q, *blocks_kv)


def back(state, gathered, sums, kv_all, tables, blocks, blocks_kv):
    length, part = gathered.shape
    hbm = pl.BlockSpec(memory_space=pl.ANY)
    vmem = pl.BlockSpec(memory_space=pltpu.VMEM)
    return pl.pallas_call(
        back_body,
        out_shape=(
            jax.ShapeDtypeStruct((length, part), jnp.bfloat16),
            jax.ShapeDtypeStruct((1, part + blocks[0].shape[0]), jnp.float32),
        ),
        in_specs=[
            pl.BlockSpec(memory_space=pltpu.SMEM),
            *[vmem] * 7,
            *[hbm] * (4 * N_Y),
        ],
        out_specs=(vmem, vmem),
        scratch_shapes=[
            pltpu.VMEM(blocks[0].shape, jnp.bfloat16),
            pltpu.VMEM((GAIN_ROWS, part), jnp.bfloat16),
            pltpu.SemaphoreType.DMA((2,)),
        ],
        compiler_params=pltpu.CompilerParams(vmem_limit_bytes=16 << 20),
        name="back",
    )(state, gathered, sums, kv_all, *tables, *blocks, *blocks_kv)


def program(token_ids, alpha_num, embed_table, norm_gain, w_query, w_key, w_value, w_out):
    bf16, f32 = jnp.bfloat16, jnp.float32
    y_index = lax.axis_index("y")
    core_index = lax.axis_index("core")
    section_index = lax.axis_index(SECTION)
    micros, length = token_ids.shape
    vocab_rows = embed_table.shape[0]
    layers = N_Y * N_CORE
    own_rows = length // N_TP
    width = w_query.shape[1]
    part = width // N_Y
    query_cols = w_query.shape[2]
    kv_cols = w_key.shape[2]
    heads_here = query_cols // HEAD_DIM

    swap = [(0, 1), (1, 0)]

    def spread(block_for, after=None):
        own = {step: block_for((y_index + step) % N_Y) for step in (0, 1, 3, 2)}
        if after is not None:
            own, _ = lax.optimization_barrier((own, after))
        for step in (1, 3, 2):
            turn = [(i, (i + step) % N_Y) for i in range(N_Y)]
            own[step] = lax.ppermute(own[step], "y", turn)
        twins = []
        for step in range(N_Y):
            twins.append(lax.ppermute(own[step], "core", swap))
        return [*[own[step] for step in range(N_Y)], *twins]

    kv_turned = jnp.concatenate([w_key[0].T, w_value[0].T], axis=0)
    routes = []
    for source in range(N_TP):
        half, place = divmod(source, N_TP // 2)
        routes.append((source, (place ^ 1) * 2 + half))
    kv_turned = lax.ppermute(kv_turned, TP, routes)
    gain = norm_gain[0]
    gain_high = lax.reduce_precision(gain, 8, 7)
    gain_mid = lax.reduce_precision(gain - gain_high, 8, 7)
    gain_low = gain - gain_high - gain_mid
    gain_rows = jnp.stack([gain_high, gain_mid, gain_low]).astype(bf16)
    kv_turned = jnp.concatenate([kv_turned, jnp.pad(gain_rows, ((0, GAIN_ROWS - 3), (0, 0)))], axis=0)

    blocks_q = spread(
        lambda block: lax.dynamic_slice_in_dim(w_query[0], block * part, part, axis=0),
    )
    blocks_kv = spread(
        lambda block: lax.dynamic_slice_in_dim(kv_turned, block * part, part, axis=1),
    )
    local_ids = token_ids - section_index * vocab_rows
    inside = (local_ids >= 0) & (local_ids < vocab_rows)
    picked = jnp.take(embed_table, jnp.clip(local_ids, 0, vocab_rows - 1), axis=0)
    picked = jnp.where(inside[:, :, None], picked, jnp.zeros((), bf16))
    feats = embed_table.shape[1]
    sent = picked.reshape(micros, N_TP, own_rows, feats).transpose(1, 0, 2, 3)
    came = lax.all_to_all(sent, TP, 0, 0, tiled=True)
    came = came.reshape(N_Y, N_TP // N_Y, micros, own_rows, feats).transpose(0, 2, 3, 1, 4)
    found = lax.all_to_all(came.reshape(layers, own_rows, part), SECTION, 0, 0, tiled=True)
    resid = jnp.sum(found.astype(f32), axis=0).astype(bf16)

    blocks_out = spread(
        lambda block: lax.dynamic_slice_in_dim(w_out[0], block * part, part, axis=1), resid
    )

    seen_q, seen_k, seen_v, seen_out, _ = lax.optimization_barrier(
        (w_query[0], w_key[0], w_value[0], w_out[0], came)
    )
    weight_local = jnp.maximum(
        jnp.max(jnp.abs(seen_q), axis=1),
        jnp.maximum(jnp.max(jnp.abs(seen_k), axis=1), jnp.max(jnp.abs(seen_v), axis=1)),
    )
    out_peak = jnp.max(jnp.abs(seen_out), axis=1).astype(f32)

    cosine, sine = rope_tables(length, HEAD_DIM)
    cosine = jnp.concatenate([cosine, cosine], axis=1)
    sine = jnp.concatenate([-sine, sine], axis=1)
    tables = (cosine, sine, cosine.T, sine.T)
    state = jnp.stack([jnp.int32(0), y_index, core_index]).astype(jnp.int32)

    kv_at = heads_here * length
    stat_at = kv_at + 2 * kv_cols

    def one_layer(state, gathered, resid):
        packed = front(state, gathered, blocks_q, blocks_kv)
        packed = lax.all_to_all(packed, "y", 0, 0, tiled=True)
        summed = jnp.sum(packed.astype(f32), axis=0)
        mean = (summed[stat_at] + summed[stat_at + 8]) / width
        inverse = lax.rsqrt(mean + norm_eps)
        kv_rows = (summed[kv_at:stat_at] * inverse[None, :]).astype(bf16)
        kv_all = copy_for_each(kv_rows, HALF)
        head_part, peaks = back(
            state, gathered, summed, kv_all, tables, blocks_out, blocks_kv
        )
        shares = lax.all_to_all(head_part.reshape(N_TP, own_rows, part), TP, 0, 0, tiled=True)
        shares, peaks, state = lax.optimization_barrier((shares, peaks, state))
        state = state + (jnp.arange(3, dtype=jnp.int32) == 0)
        mixed = jnp.sum(shares.astype(f32), axis=0)
        return (resid.astype(f32) + mixed).astype(bf16), peaks, state

    rows = weight_local.reshape(-1, part)
    both = copy_for_each(jnp.concatenate([resid, rows], axis=0), TP)
    weight_peak = jnp.max(both[:, own_rows:], axis=0).reshape(width).astype(f32)
    resid, first_peaks, state = one_layer(state, both[:, :own_rows].reshape(length, part), resid)

    def advance(carry):
        layer, resid, stored, peaks, state = carry
        gathered = copy_for_each(resid, TP).reshape(length, part)
        resid, fresh, state = one_layer(state, gathered, resid)
        layer, resid = lax.optimization_barrier((layer, resid))
        stored = lax.dynamic_update_index_in_dim(stored, resid, layer, 0)
        peaks = lax.dynamic_update_slice_in_dim(peaks, fresh, layer, 0)
        return layer + 1, resid, stored, peaks, state

    stored = jnp.zeros((layers, own_rows, part), bf16).at[0].set(resid)
    peaks = jnp.zeros((layers, part + query_cols), f32).at[0].set(first_peaks[0])
    start = (jnp.uint32(1), resid, stored, peaks, state)
    _, _, stored, peaks, _ = lax.while_loop(lambda carry: carry[0] < layers, advance, start)

    peaks = lax.all_to_all(peaks.astype(bf16), SECTION, 0, 0, tiled=True).astype(f32)
    peaks = peaks.reshape(N_Y, N_CORE, part + query_cols).max(axis=1)
    act_peak = peaks[:, :part].reshape(width)
    head_peak = peaks[0, part:]
    kept = lax.all_to_all(stored, SECTION, 0, 0, tiled=True)
    kept = kept.reshape(N_Y, N_CORE, own_rows, part).transpose(1, 2, 0, 3)
    kept = kept.reshape(micros, own_rows, width)

    alpha_exp = alpha_num[0].astype(f32) / 10.0
    scale_in = smoothing(act_peak, weight_peak, alpha_exp)
    scale_out = smoothing(head_peak, out_peak, alpha_exp)
    smooth_query, smooth_key, smooth_value = (
        (w.astype(f32) * scale_in[None, :, None]).astype(bf16) for w in (w_query, w_key, w_value)
    )
    return (kept[None], scale_in[None], scale_out[None], smooth_query, smooth_key, smooth_value)


def solution(mesh):
    split = Mesh(mesh.devices.reshape(N_Y, N_CORE, 4, 2, 2), ("y", "core", "x", "zh", "zl"))
    return jax.shard_map(
        program,
        mesh=split,
        in_specs=(
            P(),
            P(),
            P(SECTION, TP),
            P(SECTION, None),
            P(SECTION, None, TP),
            P(SECTION, None, TP),
            P(SECTION, None, TP),
            P(SECTION, TP, None),
        ),
        out_specs=(
            P(SECTION, None, TP, None),
            P(SECTION, None),
            P(SECTION, TP),
            P(SECTION, None, TP),
            P(SECTION, None, TP),
            P(SECTION, None, TP),
        ),
        check_vma=False,
    )
```

profile of v0, /device:TPU:1, one launch (start us, length us, event | category | flops | bytes accessed | tf_op | source)
XLA Modules:
  0.0 603.2 jit_solution(7479241132109710864)
XLA Ops:
  54.8 12.9 %all-to-all-done.5 = bf16[8,8,2048]{2,1,0:T(8,128)(2,1)} async-done(((bf16[8,8,2048]{2,1,0:T(8,128)(2,1)}), bf16[8,8,2048]{2,1,0:T(8,128)(2,1)}, u32[]{:S(2)}, u32[]{:S(2)}) %all-to-all-start.5) | async-done | bytes 262176 | tf_op jit(solution)/shard_map/all_to_all | solution.py:253
  81.1 45.2 %collective-permute-done.9.refs_10_ = bf16[80,2048]{1,0:T(8,128)(2,1)} collective-permute-done((bf16[80,2048]{1,0:T(8,128)(2,1)}, bf16[80,2048]{1,0:T(8,128)(2,1)}, u32[]{:S(2)}, u32[]{:S(2)}) %collective-permute-start.9) | collective-permute-done | bytes 327712 | tf_op jit(solution)/shard_map/ppermute | solution.py:220
  140.3 9.9 %all-to-all-done.6 = bf16[16,12,2048]{2,1,0:T(8,128)(2,1)} async-done(((bf16[16,12,2048]{2,1,0:T(8,128)(2,1)}), bf16[16,12,2048]{2,1,0:T(8,128)(2,1)}, u32[]{:S(2)}, u32[]{:S(2)}) %all-to-all-start.6) | async-done | bytes 786464 | tf_op jit(solution)/shard_map/all_to_all | solution.py:28
  192.4 345.7 %while.18 = (u32[]{:T(128)}, bf16[8,2048]{1,0:T(8,128)(2,1)S(1)}, bf16[8,8,2048]{2,1,0:T(8,128)(2,1)}, bf16[8,2304]{1,0:T(8,128)(2,1)S(1)}, s32[3]{0:T(128)S(1)}...) while((u32[]{:T(128)}, bf16[8,2048]{1,0:T(8,128)(2,1)S(1)}, ...), condition=%wide.region_9.10_spmd, body=%wide.region_6.9_spmd.sunk | while | flops 874891 | bytes 5648757 | solution.py:312
  192.4 11.8 %all_to_all.71 = bf16[16,8,2048]{2,1,0:T(8,128)(2,1)S(1)} all-to-all(bf16[16,8,2048]{2,1,0:T(8,128)(2,1)S(1)} %broadcast_in_dim.83), channel_id=1, replica_groups=mesh['y'=4,'core'=2,'x'=4,'zh'=2,'zl'=2] {'x','zh','zl'}, dimensions={0} | all-to-all | bytes 1048576 | tf_op jit(solution)/shard_map/while/body/all_to_all | solution.py:28
  214.8 9.6 %all_to_all.73.kv_ref = bf16[8,64,128]{2,1,0:T(8,128)(2,1)S(1)} all-to-all(bf16[8,64,128]{2,1,0:T(8,128)(2,1)S(1)} %broadcast_in_dim.84), channel_id=1, replica_groups=mesh['y'=4,'core'=2,'x'=4,'zh'=2,'zl'=2] {'x','zh'}, dimensions={0} | all-to-all | bytes 262144 | tf_op jit(solution)/shard_map/while/body/all_to_all | solution.py:28
  230.7 8.9 %all-to-all-done.3 = bf16[16,8,2048]{2,1,0:T(8,128)(2,1)S(1)} async-done(((bf16[16,8,2048]{2,1,0:T(8,128)(2,1)}), bf16[16,8,2048]{2,1,0:T(8,128)(2,1)S(1)}, u32[]{:S(2)}, u32[]{:S(2)}) %all-to-all-start.3) | async-done | bytes 524320 | tf_op jit(solution)/shard_map/while/body/all_to_all | solution.py:289
  240.4 13.0 %all_to_all.71 = bf16[16,8,2048]{2,1,0:T(8,128)(2,1)S(1)} all-to-all(bf16[16,8,2048]{2,1,0:T(8,128)(2,1)S(1)} %broadcast_in_dim.83), channel_id=1, replica_groups=mesh['y'=4,'core'=2,'x'=4,'zh'=2,'zl'=2] {'x','zh','zl'}, dimensions={0} | all-to-all | bytes 1048576 | tf_op jit(solution)/shard_map/while/body/all_to_all | solution.py:28
  264.6 9.5 %all_to_all.73.kv_ref = bf16[8,64,128]{2,1,0:T(8,128)(2,1)S(1)} all-to-all(bf16[8,64,128]{2,1,0:T(8,128)(2,1)S(1)} %broadcast_in_dim.84), channel_id=1, replica_groups=mesh['y'=4,'core'=2,'x'=4,'zh'=2,'zl'=2] {'x','zh'}, dimensions={0} | all-to-all | bytes 262144 | tf_op jit(solution)/shard_map/while/body/all_to_all | solution.py:28
  281.0 9.9 %all-to-all-done.3 = bf16[16,8,2048]{2,1,0:T(8,128)(2,1)S(1)} async-done(((bf16[16,8,2048]{2,1,0:T(8,128)(2,1)}), bf16[16,8,2048]{2,1,0:T(8,128)(2,1)S(1)}, u32[]{:S(2)}, u32[]{:S(2)}) %all-to-all-start.3) | async-done | bytes 524320 | tf_op jit(solution)/shard_map/while/body/all_to_all | solution.py:289
  291.8 11.7 %all_to_all.71 = bf16[16,8,2048]{2,1,0:T(8,128)(2,1)S(1)} all-to-all(bf16[16,8,2048]{2,1,0:T(8,128)(2,1)S(1)} %broadcast_in_dim.83), channel_id=1, replica_groups=mesh['y'=4,'core'=2,'x'=4,'zh'=2,'zl'=2] {'x','zh','zl'}, dimensions={0} | all-to-all | bytes 1048576 | tf_op jit(solution)/shard_map/while/body/all_to_all | solution.py:28
  314.3 9.6 %all_to_all.73.kv_ref = bf16[8,64,128]{2,1,0:T(8,128)(2,1)S(1)} all-to-all(bf16[8,64,128]{2,1,0:T(8,128)(2,1)S(1)} %broadcast_in_dim.84), channel_id=1, replica_groups=mesh['y'=4,'core'=2,'x'=4,'zh'=2,'zl'=2] {'x','zh'}, dimensions={0} | all-to-all | bytes 262144 | tf_op jit(solution)/shard_map/while/body/all_to_all | solution.py:28
  330.8 8.9 %all-to-all-done.3 = bf16[16,8,2048]{2,1,0:T(8,128)(2,1)S(1)} async-done(((bf16[16,8,2048]{2,1,0:T(8,128)(2,1)}), bf16[16,8,2048]{2,1,0:T(8,128)(2,1)S(1)}, u32[]{:S(2)}, u32[]{:S(2)}) %all-to-all-start.3) | async-done | bytes 524320 | tf_op jit(solution)/shard_map/while/body/all_to_all | solution.py:289
  340.6 11.9 %all_to_all.71 = bf16[16,8,2048]{2,1,0:T(8,128)(2,1)S(1)} all-to-all(bf16[16,8,2048]{2,1,0:T(8,128)(2,1)S(1)} %broadcast_in_dim.83), channel_id=1, replica_groups=mesh['y'=4,'core'=2,'x'=4,'zh'=2,'zl'=2] {'x','zh','zl'}, dimensions={0} | all-to-all | bytes 1048576 | tf_op jit(solution)/shard_map/while/body/all_to_all | solution.py:28
  363.4 9.9 %all_to_all.73.kv_ref = bf16[8,64,128]{2,1,0:T(8,128)(2,1)S(1)} all-to-all(bf16[8,64,128]{2,1,0:T(8,128)(2,1)S(1)} %broadcast_in_dim.84), channel_id=1, replica_groups=mesh['y'=4,'core'=2,'x'=4,'zh'=2,'zl'=2] {'x','zh'}, dimensions={0} | all-to-all | bytes 262144 | tf_op jit(solution)/shard_map/while/body/all_to_all | solution.py:28
  389.9 12.2 %all_to_all.71 = bf16[16,8,2048]{2,1,0:T(8,128)(2,1)S(1)} all-to-all(bf16[16,8,2048]{2,1,0:T(8,128)(2,1)S(1)} %broadcast_in_dim.83), channel_id=1, replica_groups=mesh['y'=4,'core'=2,'x'=4,'zh'=2,'zl'=2] {'x','zh','zl'}, dimensions={0} | all-to-all | bytes 1048576 | tf_op jit(solution)/shard_map/while/body/all_to_all | solution.py:28
  413.2 9.2 %all_to_all.73.kv_ref = bf16[8,64,128]{2,1,0:T(8,128)(2,1)S(1)} all-to-all(bf16[8,64,128]{2,1,0:T(8,128)(2,1)S(1)} %broadcast_in_dim.84), channel_id=1, replica_groups=mesh['y'=4,'core'=2,'x'=4,'zh'=2,'zl'=2] {'x','zh'}, dimensions={0} | all-to-all | bytes 262144 | tf_op jit(solution)/shard_map/while/body/all_to_all | solution.py:28
  439.0 11.9 %all_to_all.71 = bf16[16,8,2048]{2,1,0:T(8,128)(2,1)S(1)} all-to-all(bf16[16,8,2048]{2,1,0:T(8,128)(2,1)S(1)} %broadcast_in_dim.83), channel_id=1, replica_groups=mesh['y'=4,'core'=2,'x'=4,'zh'=2,'zl'=2] {'x','zh','zl'}, dimensions={0} | all-to-all | bytes 1048576 | tf_op jit(solution)/shard_map/while/body/all_to_all | solution.py:28
  461.8 9.9 %all_to_all.73.kv_ref = bf16[8,64,128]{2,1,0:T(8,128)(2,1)S(1)} all-to-all(bf16[8,64,128]{2,1,0:T(8,128)(2,1)S(1)} %broadcast_in_dim.84), channel_id=1, replica_groups=mesh['y'=4,'core'=2,'x'=4,'zh'=2,'zl'=2] {'x','zh'}, dimensions={0} | all-to-all | bytes 262144 | tf_op jit(solution)/shard_map/while/body/all_to_all | solution.py:28
  478.7 9.2 %all-to-all-done.3 = bf16[16,8,2048]{2,1,0:T(8,128)(2,1)S(1)} async-done(((bf16[16,8,2048]{2,1,0:T(8,128)(2,1)}), bf16[16,8,2048]{2,1,0:T(8,128)(2,1)S(1)}, u32[]{:S(2)}, u32[]{:S(2)}) %all-to-all-start.3) | async-done | bytes 524320 | tf_op jit(solution)/shard_map/while/body/all_to_all | solution.py:289
  488.7 11.9 %all_to_all.71 = bf16[16,8,2048]{2,1,0:T(8,128)(2,1)S(1)} all-to-all(bf16[16,8,2048]{2,1,0:T(8,128)(2,1)S(1)} %broadcast_in_dim.83), channel_id=1, replica_groups=mesh['y'=4,'core'=2,'x'=4,'zh'=2,'zl'=2] {'x','zh','zl'}, dimensions={0} | all-to-all | bytes 1048576 | tf_op jit(solution)/shard_map/while/body/all_to_all | solution.py:28
  511.5 9.8 %all_to_all.73.kv_ref = bf16[8,64,128]{2,1,0:T(8,128)(2,1)S(1)} all-to-all(bf16[8,64,128]{2,1,0:T(8,128)(2,1)S(1)} %broadcast_in_dim.84), channel_id=1, replica_groups=mesh['y'=4,'core'=2,'x'=4,'zh'=2,'zl'=2] {'x','zh'}, dimensions={0} | all-to-all | bytes 262144 | tf_op jit(solution)/shard_map/while/body/all_to_all | solution.py:28
  528.2 9.1 %all-to-all-done.3 = bf16[16,8,2048]{2,1,0:T(8,128)(2,1)S(1)} async-done(((bf16[16,8,2048]{2,1,0:T(8,128)(2,1)}), bf16[16,8,2048]{2,1,0:T(8,128)(2,1)S(1)}, u32[]{:S(2)}, u32[]{:S(2)}) %all-to-all-start.3) | async-done | bytes 524320 | tf_op jit(solution)/shard_map/while/body/all_to_all | solution.py:289
  539.9 46.6 %all-to-all-start.11 = ((bf16[8,2,1152]{2,1,0:T(2,128)(2,1)}), bf16[8,2,1152]{2,1,0:T(2,128)(2,1)S(1)}, u32[]{:S(2)}, u32[]{:S(2)}) async-start(bf16[8,2,1152]{2,1,0:T(2,128)(2,1)} %reshape.276), calls=%async_computation.11 | async-start | bytes 73728 | tf_op jit(solution)/shard_map/all_to_all | solution.py:314
  (234 shorter events, 288.4 us)
Async XLA Ops:
  2.9 36.4 %collective-permute-start.7 = (bf16[64,8192]{1,0:T(8,128)(2,1)}, bf16[64,8192]{1,0:T(8,128)(2,1)}, u32[]{:S(2)}, u32[]{:S(2)}) collective-permute-start(bf16[64,8192]{1,0:T(8,128)(2,1)} %pad_maximum_fusion), channel_id=1, source_target_pairs={{0,2},{1,0},{2,6},{3,4},{4,10},{5,8},{6,14},{7,12},{8,3},{9,1},{10... | collective-permute-start | bytes 3145736 | tf_op jit(solution)/shard_map/ppermute | solution.py:231
  11.1 38.2 %collective-permute-start.2 = (bf16[2048,256]{1,0:T(8,128)(2,1)S(1)}, bf16[2048,256]{1,0:T(8,128)(2,1)S(1)}, u32[]{:S(2)}, u32[]{:S(2)}) collective-permute-start(bf16[2048,256]{1,0:T(8,128)(2,1)S(1)} %get-tuple-element.468), channel_id=1, source_target_pairs={{0,96},{32,0},{64,32},{96,64},{1,97},{33,1},{65,33},{97,65},{2,98}... | collective-permute-start | bytes 3145736 | tf_op jit(solution)/shard_map/ppermute | solution.py:220
  13.8 54.9 %collective-permute-start.1 = (bf16[2048,256]{1,0:T(8,128)(2,1)}, bf16[2048,256]{1,0:T(8,128)(2,1)}, u32[]{:S(2)}, u32[]{:S(2)}) collective-permute-start(bf16[2048,256]{1,0:T(8,128)(2,1)} %get-tuple-element.469), channel_id=1, source_target_pairs={{0,64},{32,96},{64,0},{96,32},{1,65},{33,97},{65,1},{97,33},{2,66}... | collective-permute-start | bytes 3145736 | tf_op jit(solution)/shard_map/ppermute | solution.py:220
  14.2 57.3 %collective-permute-start = (bf16[2048,256]{1,0:T(8,128)(2,1)}, bf16[2048,256]{1,0:T(8,128)(2,1)}, u32[]{:S(2)}, u32[]{:S(2)}) collective-permute-start(bf16[2048,256]{1,0:T(8,128)(2,1)} %get-tuple-element.470), channel_id=1, source_target_pairs={{0,32},{32,64},{64,96},{96,0},{1,33},{33,65},{65,97},{97,1},{2,34}... | collective-permute-start | bytes 3145736 | tf_op jit(solution)/shard_map/ppermute | solution.py:220
  14.8 59.4 %collective-permute-start.3 = (bf16[2048,256]{1,0:T(8,128)(2,1)S(1)}, bf16[2048,256]{1,0:T(8,128)(2,1)}, u32[]{:S(2)}, u32[]{:S(2)}) collective-permute-start(bf16[2048,256]{1,0:T(8,128)(2,1)S(1)} %get-tuple-element.714.refs_0_), channel_id=1, source_target_pairs={{0,16},{16,0},{1,17},{17,1},{2,18},{18,2},{3,19},{19,3},{4,20},{20... | collective-permute-start | bytes 3145736 | tf_op jit(solution)/shard_map/ppermute | solution.py:223
  23.5 13.0 %all-to-all-start.4 = ((bf16[16,2,8,512]{3,2,1,0:T(8,128)(2,1)}), bf16[16,2,8,512]{3,2,1,0:T(8,128)(2,1)S(1)}, u32[]{:S(2)}, u32[]{:S(2)}) async-start(bf16[16,2,8,512]{3,2,1,0:T(8,128)(2,1)} %fusion.13), calls=%async_computation.4 | async-start | bytes 524288 | tf_op jit(solution)/shard_map/all_to_all | solution.py:251
  41.5 32.8 %collective-permute-start.10 = (bf16[80,2048]{1,0:T(8,128)(2,1)}, bf16[80,2048]{1,0:T(8,128)(2,1)}, u32[]{:S(2)}, u32[]{:S(2)}) collective-permute-start(bf16[80,2048]{1,0:T(8,128)(2,1)} %get-tuple-element.472), channel_id=1, source_target_pairs={{0,96},{32,0},{64,32},{96,64},{1,97},{33,1},{65,33},{97,65},{2,98}... | collective-permute-start | bytes 983048 | tf_op jit(solution)/shard_map/ppermute | solution.py:220
  43.4 24.2 %all-to-all-start.5 = ((bf16[8,8,2048]{2,1,0:T(8,128)(2,1)}), bf16[8,8,2048]{2,1,0:T(8,128)(2,1)}, u32[]{:S(2)}, u32[]{:S(2)}) async-start(bf16[8,8,2048]{2,1,0:T(8,128)(2,1)} %reshape.256), calls=%async_computation.5 | async-start | bytes 524288 | tf_op jit(solution)/shard_map/all_to_all | solution.py:253
  49.3 26.2 %collective-permute-start.8 = (bf16[80,2048]{1,0:T(8,128)(2,1)}, bf16[80,2048]{1,0:T(8,128)(2,1)}, u32[]{:S(2)}, u32[]{:S(2)}) collective-permute-start(bf16[80,2048]{1,0:T(8,128)(2,1)} %get-tuple-element.474), channel_id=1, source_target_pairs={{0,32},{32,64},{64,96},{96,0},{1,33},{33,65},{65,97},{97,1},{2,34}... | collective-permute-start | bytes 983048 | tf_op jit(solution)/shard_map/ppermute | solution.py:220
  68.7 65.8 %collective-permute-start.15 = (bf16[256,2048]{1,0:T(8,128)(2,1)}, bf16[256,2048]{1,0:T(8,128)(2,1)}, u32[]{:S(2)}, u32[]{:S(2)}) collective-permute-start(bf16[256,2048]{1,0:T(8,128)(2,1)} %get-tuple-element.222), channel_id=1, source_target_pairs={{0,32},{32,64},{64,96},{96,0},{1,33},{33,65},{65,97},{97,1},{2,34}... | collective-permute-start | bytes 3145736 | tf_op jit(solution)/shard_map/ppermute | solution.py:220
  71.5 63.9 %collective-permute-start.16 = (bf16[256,2048]{1,0:T(8,128)(2,1)}, bf16[256,2048]{1,0:T(8,128)(2,1)}, u32[]{:S(2)}, u32[]{:S(2)}) collective-permute-start(bf16[256,2048]{1,0:T(8,128)(2,1)} %get-tuple-element.223), channel_id=1, source_target_pairs={{0,64},{32,96},{64,0},{96,32},{1,65},{33,97},{65,1},{97,33},{2,66}... | collective-permute-start | bytes 3145736 | tf_op jit(solution)/shard_map/ppermute | solution.py:220
  74.3 61.2 %collective-permute-start.17 = (bf16[256,2048]{1,0:T(8,128)(2,1)}, bf16[256,2048]{1,0:T(8,128)(2,1)}, u32[]{:S(2)}, u32[]{:S(2)}) collective-permute-start(bf16[256,2048]{1,0:T(8,128)(2,1)} %get-tuple-element.224), channel_id=1, source_target_pairs={{0,96},{32,0},{64,32},{96,64},{1,97},{33,1},{65,33},{97,65},{2,98}... | collective-permute-start | bytes 3145736 | tf_op jit(solution)/shard_map/ppermute | solution.py:220
  74.3 52.0 %collective-permute-start.9 = (bf16[80,2048]{1,0:T(8,128)(2,1)}, bf16[80,2048]{1,0:T(8,128)(2,1)}, u32[]{:S(2)}, u32[]{:S(2)}) collective-permute-start(bf16[80,2048]{1,0:T(8,128)(2,1)} %get-tuple-element.475), channel_id=1, source_target_pairs={{0,64},{32,96},{64,0},{96,32},{1,65},{33,97},{65,1},{97,33},{2,66}... | collective-permute-start | bytes 983048 | tf_op jit(solution)/shard_map/ppermute | solution.py:220
  75.5 52.6 %collective-permute-start.11 = (bf16[80,2048]{1,0:T(8,128)(2,1)S(1)}, bf16[80,2048]{1,0:T(8,128)(2,1)}, u32[]{:S(2)}, u32[]{:S(2)}) collective-permute-start(bf16[80,2048]{1,0:T(8,128)(2,1)S(1)} %get-tuple-element.722.refs_8_), channel_id=1, source_target_pairs={{0,16},{16,0},{1,17},{17,1},{2,18},{18,2},{3,19},{19,3},{4,20},{20... | collective-permute-start | bytes 983048 | tf_op jit(solution)/shard_map/ppermute | solution.py:223
  126.3 13.5 %collective-permute-start.6 = (bf16[2048,256]{1,0:T(8,128)(2,1)S(1)}, bf16[2048,256]{1,0:T(8,128)(2,1)}, u32[]{:S(2)}, u32[]{:S(2)}) collective-permute-start(bf16[2048,256]{1,0:T(8,128)(2,1)S(1)} %collective-permute-done.2.refs_3_), channel_id=1, source_target_pairs={{0,16},{16,0},{1,17},{17,1},{2,18},{18,2},{3,19},{19,3},{4,20},{20... | collective-permute-start | bytes 3145736 | tf_op jit(solution)/shard_map/ppermute | solution.py:223
  129.3 20.9 %all-to-all-start.6 = ((bf16[16,12,2048]{2,1,0:T(8,128)(2,1)}), bf16[16,12,2048]{2,1,0:T(8,128)(2,1)}, u32[]{:S(2)}, u32[]{:S(2)}) async-start(bf16[16,12,2048]{2,1,0:T(8,128)(2,1)} %broadcast_in_dim.75), calls=%async_computation.6 | async-start | bytes 2097152 | tf_op jit(solution)/shard_map/all_to_all | solution.py:28
  135.4 15.9 %collective-permute-start.4 = (bf16[2048,256]{1,0:T(8,128)(2,1)}, bf16[2048,256]{1,0:T(8,128)(2,1)}, u32[]{:S(2)}, u32[]{:S(2)}) collective-permute-start(bf16[2048,256]{1,0:T(8,128)(2,1)} %collective-permute-done.refs_1_), channel_id=1, source_target_pairs={{0,16},{16,0},{1,17},{17,1},{2,18},{18,2},{3,19},{19,3},{4,20},{20... | collective-permute-start | bytes 3145736 | tf_op jit(solution)/shard_map/ppermute | solution.py:223
  139.0 32.3 %collective-permute-start.18 = (bf16[256,2048]{1,0:T(8,128)(2,1)S(1)}, bf16[256,2048]{1,0:T(8,128)(2,1)}, u32[]{:S(2)}, u32[]{:S(2)}) collective-permute-start(bf16[256,2048]{1,0:T(8,128)(2,1)S(1)} %get-tuple-element.734.refs_0_), channel_id=1, source_target_pairs={{0,16},{16,0},{1,17},{17,1},{2,18},{18,2},{3,19},{19,3},{4,20},{20... | collective-permute-start | bytes 3145736 | tf_op jit(solution)/shard_map/ppermute | solution.py:223
  139.4 36.1 %collective-permute-start.19 = (bf16[256,2048]{1,0:T(8,128)(2,1)}, bf16[256,2048]{1,0:T(8,128)(2,1)}, u32[]{:S(2)}, u32[]{:S(2)}) collective-permute-start(bf16[256,2048]{1,0:T(8,128)(2,1)} %collective-permute-done.15.refs_1_), channel_id=1, source_target_pairs={{0,16},{16,0},{1,17},{17,1},{2,18},{18,2},{3,19},{19,3},{4,20},{20... | collective-permute-start | bytes 3145736 | tf_op jit(solution)/shard_map/ppermute | solution.py:223
  139.8 35.7 %collective-permute-start.20 = (bf16[256,2048]{1,0:T(8,128)(2,1)}, bf16[256,2048]{1,0:T(8,128)(2,1)}, u32[]{:S(2)}, u32[]{:S(2)}) collective-permute-start(bf16[256,2048]{1,0:T(8,128)(2,1)} %collective-permute-done.16.refs_2_), channel_id=1, source_target_pairs={{0,16},{16,0},{1,17},{17,1},{2,18},{18,2},{3,19},{19,3},{4,20},{20... | collective-permute-start | bytes 3145736 | tf_op jit(solution)/shard_map/ppermute | solution.py:223
  139.9 35.6 %collective-permute-start.21 = (bf16[256,2048]{1,0:T(8,128)(2,1)}, bf16[256,2048]{1,0:T(8,128)(2,1)}, u32[]{:S(2)}, u32[]{:S(2)}) collective-permute-start(bf16[256,2048]{1,0:T(8,128)(2,1)} %collective-permute-done.17.refs_3_), channel_id=1, source_target_pairs={{0,16},{16,0},{1,17},{17,1},{2,18},{18,2},{3,19},{19,3},{4,20},{20... | collective-permute-start | bytes 3145736 | tf_op jit(solution)/shard_map/ppermute | solution.py:223
  277.5 13.5 %all-to-all-start.3 = ((bf16[16,8,2048]{2,1,0:T(8,128)(2,1)}), bf16[16,8,2048]{2,1,0:T(8,128)(2,1)S(1)}, u32[]{:S(2)}, u32[]{:S(2)}) async-start(bf16[16,8,2048]{2,1,0:T(8,128)(2,1)} %bitcast.73), calls=%async_computation.3 | async-start | bytes 1048576 | tf_op jit(solution)/shard_map/while/body/all_to_all | solution.py:289
  475.1 12.8 %all-to-all-start.3 = ((bf16[16,8,2048]{2,1,0:T(8,128)(2,1)}), bf16[16,8,2048]{2,1,0:T(8,128)(2,1)S(1)}, u32[]{:S(2)}, u32[]{:S(2)}) async-start(bf16[16,8,2048]{2,1,0:T(8,128)(2,1)} %bitcast.73), calls=%async_computation.3 | async-start | bytes 1048576 | tf_op jit(solution)/shard_map/while/body/all_to_all | solution.py:289
  539.9 51.3 %all-to-all-start.11 = ((bf16[8,2,1152]{2,1,0:T(2,128)(2,1)}), bf16[8,2,1152]{2,1,0:T(2,128)(2,1)S(1)}, u32[]{:S(2)}, u32[]{:S(2)}) async-start(bf16[8,2,1152]{2,1,0:T(2,128)(2,1)} %reshape.276), calls=%async_computation.11 | async-start | bytes 73728 | tf_op jit(solution)/shard_map/all_to_all | solution.py:314
  (22 other events, 343.3 us)
where the time goes:
time: 607 us; the launch traced here: 603 us
  blocking collectives  211 us (35%)
  waiting for transfers between devices  160 us (26%)
  starting transfers between devices  130 us (21%)
  Pallas kernels  45.3 us (7%)
  local copies, waits for them, and re-layouts  28.8 us (5%)
  other arithmetic  25.8 us (4%)
    all_to_all x14, blocking collectives, copy_for_each(): lax.all_to_all(jnp.broadcast_to(value[None], (count, *value.shape)), axis...  152 us
    all_to_all x8, waiting for transfers between devices, one_layer(): lax.all_to_all(head_part.reshape(N_TP, own_rows, part), TP, 0, 0, tiled=T...  69.9 us
    all_to_all x7, blocking collectives, one_layer(): packed = lax.all_to_all(packed, 'y', 0, 0, tiled=True)  59.3 us
    all_to_all x1, starting transfers between devices, program(): lax.all_to_all(peaks.astype(bf16), SECTION, 0, 0, tiled=True).astype(f32)  46.6 us
    ppermute x9, waiting for transfers between devices, spread(): own[step] = lax.ppermute(own[step], 'y', turn)  45.2 us
    all_to_all x8, starting transfers between devices, one_layer(): lax.all_to_all(head_part.reshape(N_TP, own_rows, part), TP, 0, 0, tiled=T...  28.7 us
    pallas_call x8, Pallas kernels, back(): pl.pallas_call(back_body, out_shape=(jax.ShapeDtypeStruct((length, part),...  25.9 us
    pallas_call x8, Pallas kernels, front(): pl.pallas_call(front_body, out_shape=jax.ShapeDtypeStruct((N_Y, rows, len...  19.4 us
  transfers between devices with their start and end apart: 37, of which 18 were waited for; matrix products, arithmetic and copies ran while one was open for 7% of the time, Pallas kernels for 1%

commit v1 on v0

--- a/solution.py
+++ b/solution.py
@@ -287,29 +287,32 @@
             state, gathered, summed, kv_all, tables, blocks_out, blocks_kv
         )
         shares = lax.all_to_all(head_part.reshape(N_TP, own_rows, part), TP, 0, 0, tiled=True)
-        shares, peaks, state = lax.optimization_barrier((shares, peaks, state))
-        state = state + (jnp.arange(3, dtype=jnp.int32) == 0)
+        shares, peaks = lax.optimization_barrier((shares, peaks))
         mixed = jnp.sum(shares.astype(f32), axis=0)
-        return (resid.astype(f32) + mixed).astype(bf16), peaks, state
+        return (resid.astype(f32) + mixed).astype(bf16), peaks
 
     rows = weight_local.reshape(-1, part)
     both = copy_for_each(jnp.concatenate([resid, rows], axis=0), TP)
     weight_peak = jnp.max(both[:, own_rows:], axis=0).reshape(width).astype(f32)
-    resid, first_peaks, state = one_layer(state, both[:, :own_rows].reshape(length, part), resid)
+    resid, first_peaks = one_layer(
+        state, both[:, :own_rows].reshape(length, part), resid
+    )
 
     def advance(carry):
-        layer, resid, stored, peaks, state = carry
+        layer, resid, stored, peaks = carry
+        now = state + layer.astype(jnp.int32) * (jnp.arange(3, dtype=jnp.int32) == 0)
+        resid, now = lax.optimization_barrier((resid, now))
         gathered = copy_for_each(resid, TP).reshape(length, part)
-        resid, fresh, state = one_layer(state, gathered, resid)
+        resid, fresh = one_layer(now, gathered, resid)
         layer, resid = lax.optimization_barrier((layer, resid))
         stored = lax.dynamic_update_index_in_dim(stored, resid, layer, 0)
         peaks = lax.dynamic_update_slice_in_dim(peaks, fresh, layer, 0)
-        return layer + 1, resid, stored, peaks, state
+        return layer + 1, resid, stored, peaks
 
     stored = jnp.zeros((layers, own_rows, part), bf16).at[0].set(resid)
     peaks = jnp.zeros((layers, part + query_cols), f32).at[0].set(first_peaks[0])
-    start = (jnp.uint32(1), resid, stored, peaks, state)
-    _, _, stored, peaks, _ = lax.while_loop(lambda carry: carry[0] < layers, advance, start)
+    start = (jnp.uint32(1), resid, stored, peaks)
+    _, _, stored, peaks = lax.while_loop(lambda carry: carry[0] < layers, advance, start)
 
     peaks = lax.all_to_all(peaks.astype(bf16), SECTION, 0, 0, tiled=True).astype(f32)
     peaks = peaks.reshape(N_Y, N_CORE, part + query_cols).max(axis=1)

time: 607 us -> 596 us (0.982)
  blocking collectives: 211 us -> 296 us
  waiting for transfers between devices: 160 us -> 95.9 us
  starting transfers between devices: 130 us -> 105 us
    all_to_all x0 -> x7, blocking collectives: none -> 82.7 us  [one_layer(): lax.all_to_all(head_part.reshape(N_TP, own_rows, part), TP, 0, 0, tiled=T...]
    all_to_all x8 -> x1, waiting for transfers between devices: 69.9 us -> 5.97 us  [one_layer(): lax.all_to_all(head_part.reshape(N_TP, own_rows, part), TP, 0, 0, tiled=T...]
    all_to_all x8 -> x1, starting transfers between devices: 28.7 us -> 3.59 us  [one_layer(): lax.all_to_all(head_part.reshape(N_TP, own_rows, part), TP, 0, 0, tiled=T...]
  transfers between devices with their start and end apart: 37 -> 30, of which waited for: 18 -> 11; matrix products, arithmetic and copies ran while one was open for 7% -> 7% of each run, Pallas kernels for 1% -> 1%
where the time goes in v1:
time: 596 us; the launch traced here: 593 us
  blocking collectives  296 us (50%)
  starting transfers between devices  105 us (18%)
  waiting for transfers between devices  95.9 us (16%)
  Pallas kernels  39.7 us (7%)
  local copies, waits for them, and re-layouts  28.8 us (5%)
  other arithmetic  25.7 us (4%)
    all_to_all x14, blocking collectives, copy_for_each(): lax.all_to_all(jnp.broadcast_to(value[None], (count, *value.shape)), axis...  154 us
    all_to_all x7, blocking collectives, one_layer(): lax.all_to_all(head_part.reshape(N_TP, own_rows, part), TP, 0, 0, tiled=T...  82.7 us
    all_to_all x7, blocking collectives, one_layer(): packed = lax.all_to_all(packed, 'y', 0, 0, tiled=True)  59.2 us
    all_to_all x1, starting transfers between devices, program(): lax.all_to_all(peaks.astype(bf16), SECTION, 0, 0, tiled=True).astype(f32)  46.6 us
    ppermute x9, waiting for transfers between devices, spread(): own[step] = lax.ppermute(own[step], 'y', turn)  45.2 us
    pallas_call x8, Pallas kernels, back(): pl.pallas_call(back_body, out_shape=(jax.ShapeDtypeStruct((length, part),...  20.3 us
    pallas_call x8, Pallas kernels, front(): pl.pallas_call(front_body, out_shape=jax.ShapeDtypeStruct((N_Y, rows, len...  19.4 us
    all_to_all x2, waiting for transfers between devices, copy_for_each(): lax.all_to_all(jnp.broadcast_to(value[None], (count, *value.shape)), axis...  14.1 us
  transfers between devices with their start and end apart: 30, of which 11 were waited for; matrix products, arithmetic and copies ran while one was open for 7% of the time, Pallas kernels for 1%

profile of v1, /device:TPU:1, one launch (start us, length us, event | category | flops | bytes accessed | tf_op | source)
XLA Modules:
  0.0 593.3 jit_solution(2720350236448694311)
XLA Ops:
  54.8 12.9 %all-to-all-done.5 = bf16[8,8,2048]{2,1,0:T(8,128)(2,1)} async-done(((bf16[8,8,2048]{2,1,0:T(8,128)(2,1)}), bf16[8,8,2048]{2,1,0:T(8,128)(2,1)}, u32[]{:S(2)}, u32[]{:S(2)}) %all-to-all-start.5) | async-done | bytes 262176 | tf_op jit(solution)/shard_map/all_to_all | solution.py:253
  81.1 45.2 %collective-permute-done.9.refs_10_ = bf16[80,2048]{1,0:T(8,128)(2,1)} collective-permute-done((bf16[80,2048]{1,0:T(8,128)(2,1)}, bf16[80,2048]{1,0:T(8,128)(2,1)}, u32[]{:S(2)}, u32[]{:S(2)}) %collective-permute-start.9) | collective-permute-done | bytes 327712 | tf_op jit(solution)/shard_map/ppermute | solution.py:220
  140.3 9.9 %all-to-all-done.6 = bf16[16,12,2048]{2,1,0:T(8,128)(2,1)} async-done(((bf16[16,12,2048]{2,1,0:T(8,128)(2,1)}), bf16[16,12,2048]{2,1,0:T(8,128)(2,1)}, u32[]{:S(2)}, u32[]{:S(2)}) %all-to-all-start.6) | async-done | bytes 786464 | tf_op jit(solution)/shard_map/all_to_all | solution.py:28
  192.4 335.9 %while.16 = (u32[]{:T(128)}, bf16[8,2048]{1,0:T(8,128)(2,1)S(1)}, bf16[8,8,2048]{2,1,0:T(8,128)(2,1)}, bf16[8,2304]{1,0:T(8,128)(2,1)S(1)}, s32[3]{0:T(128)S(1)}...) while((u32[]{:T(128)}, bf16[8,2048]{1,0:T(8,128)(2,1)S(1)}, ...), condition=%wide.region_9.10_spmd, body=%wide.region_6.9_spmd.sunk | while | flops 874892 | bytes 5124449 | solution.py:315
  192.4 11.8 %all_to_all.71 = bf16[16,8,2048]{2,1,0:T(8,128)(2,1)S(1)} all-to-all(bf16[16,8,2048]{2,1,0:T(8,128)(2,1)S(1)} %broadcast_in_dim.83), channel_id=1, replica_groups=mesh['y'=4,'core'=2,'x'=4,'zh'=2,'zl'=2] {'x','zh','zl'}, dimensions={0} | all-to-all | bytes 1048576 | tf_op jit(solution)/shard_map/while/body/all_to_all | solution.py:28
  226.3 11.6 %all_to_all.74 = bf16[16,8,2048]{2,1,0:T(8,128)(2,1)S(1)} all-to-all(bf16[16,8,2048]{2,1,0:T(8,128)(2,1)S(1)} %bitcast.76), channel_id=1, replica_groups=mesh['y'=4,'core'=2,'x'=4,'zh'=2,'zl'=2] {'x','zh','zl'}, dimensions={0} | all-to-all | bytes 1048576 | tf_op jit(solution)/shard_map/while/body/all_to_all | solution.py:289
  238.7 13.2 %all_to_all.71 = bf16[16,8,2048]{2,1,0:T(8,128)(2,1)S(1)} all-to-all(bf16[16,8,2048]{2,1,0:T(8,128)(2,1)S(1)} %broadcast_in_dim.83), channel_id=1, replica_groups=mesh['y'=4,'core'=2,'x'=4,'zh'=2,'zl'=2] {'x','zh','zl'}, dimensions={0} | all-to-all | bytes 1048576 | tf_op jit(solution)/shard_map/while/body/all_to_all | solution.py:28
  275.1 11.7 %all_to_all.74 = bf16[16,8,2048]{2,1,0:T(8,128)(2,1)S(1)} all-to-all(bf16[16,8,2048]{2,1,0:T(8,128)(2,1)S(1)} %bitcast.76), channel_id=1, replica_groups=mesh['y'=4,'core'=2,'x'=4,'zh'=2,'zl'=2] {'x','zh','zl'}, dimensions={0} | all-to-all | bytes 1048576 | tf_op jit(solution)/shard_map/while/body/all_to_all | solution.py:289
  287.6 12.1 %all_to_all.71 = bf16[16,8,2048]{2,1,0:T(8,128)(2,1)S(1)} all-to-all(bf16[16,8,2048]{2,1,0:T(8,128)(2,1)S(1)} %broadcast_in_dim.83), channel_id=1, replica_groups=mesh['y'=4,'core'=2,'x'=4,'zh'=2,'zl'=2] {'x','zh','zl'}, dimensions={0} | all-to-all | bytes 1048576 | tf_op jit(solution)/shard_map/while/body/all_to_all | solution.py:28
  310.6 9.9 %all_to_all.73.kv_ref = bf16[8,64,128]{2,1,0:T(8,128)(2,1)S(1)} all-to-all(bf16[8,64,128]{2,1,0:T(8,128)(2,1)S(1)} %broadcast_in_dim.84), channel_id=1, replica_groups=mesh['y'=4,'core'=2,'x'=4,'zh'=2,'zl'=2] {'x','zh'}, dimensions={0} | all-to-all | bytes 262144 | tf_op jit(solution)/shard_map/while/body/all_to_all | solution.py:28
  323.1 11.6 %all_to_all.74 = bf16[16,8,2048]{2,1,0:T(8,128)(2,1)S(1)} all-to-all(bf16[16,8,2048]{2,1,0:T(8,128)(2,1)S(1)} %bitcast.76), channel_id=1, replica_groups=mesh['y'=4,'core'=2,'x'=4,'zh'=2,'zl'=2] {'x','zh','zl'}, dimensions={0} | all-to-all | bytes 1048576 | tf_op jit(solution)/shard_map/while/body/all_to_all | solution.py:289
  335.5 11.9 %all_to_all.71 = bf16[16,8,2048]{2,1,0:T(8,128)(2,1)S(1)} all-to-all(bf16[16,8,2048]{2,1,0:T(8,128)(2,1)S(1)} %broadcast_in_dim.83), channel_id=1, replica_groups=mesh['y'=4,'core'=2,'x'=4,'zh'=2,'zl'=2] {'x','zh','zl'}, dimensions={0} | all-to-all | bytes 1048576 | tf_op jit(solution)/shard_map/while/body/all_to_all | solution.py:28
  358.2 10.3 %all_to_all.73.kv_ref = bf16[8,64,128]{2,1,0:T(8,128)(2,1)S(1)} all-to-all(bf16[8,64,128]{2,1,0:T(8,128)(2,1)S(1)} %broadcast_in_dim.84), channel_id=1, replica_groups=mesh['y'=4,'core'=2,'x'=4,'zh'=2,'zl'=2] {'x','zh'}, dimensions={0} | all-to-all | bytes 262144 | tf_op jit(solution)/shard_map/while/body/all_to_all | solution.py:28
  371.1 11.7 %all_to_all.74 = bf16[16,8,2048]{2,1,0:T(8,128)(2,1)S(1)} all-to-all(bf16[16,8,2048]{2,1,0:T(8,128)(2,1)S(1)} %bitcast.76), channel_id=1, replica_groups=mesh['y'=4,'core'=2,'x'=4,'zh'=2,'zl'=2] {'x','zh','zl'}, dimensions={0} | all-to-all | bytes 1048576 | tf_op jit(solution)/shard_map/while/body/all_to_all | solution.py:289
  383.6 12.7 %all_to_all.71 = bf16[16,8,2048]{2,1,0:T(8,128)(2,1)S(1)} all-to-all(bf16[16,8,2048]{2,1,0:T(8,128)(2,1)S(1)} %broadcast_in_dim.83), channel_id=1, replica_groups=mesh['y'=4,'core'=2,'x'=4,'zh'=2,'zl'=2] {'x','zh','zl'}, dimensions={0} | all-to-all | bytes 1048576 | tf_op jit(solution)/shard_map/while/body/all_to_all | solution.py:28
  407.4 9.6 %all_to_all.73.kv_ref = bf16[8,64,128]{2,1,0:T(8,128)(2,1)S(1)} all-to-all(bf16[8,64,128]{2,1,0:T(8,128)(2,1)S(1)} %broadcast_in_dim.84), channel_id=1, replica_groups=mesh['y'=4,'core'=2,'x'=4,'zh'=2,'zl'=2] {'x','zh'}, dimensions={0} | all-to-all | bytes 262144 | tf_op jit(solution)/shard_map/while/body/all_to_all | solution.py:28
  419.6 11.6 %all_to_all.74 = bf16[16,8,2048]{2,1,0:T(8,128)(2,1)S(1)} all-to-all(bf16[16,8,2048]{2,1,0:T(8,128)(2,1)S(1)} %bitcast.76), channel_id=1, replica_groups=mesh['y'=4,'core'=2,'x'=4,'zh'=2,'zl'=2] {'x','zh','zl'}, dimensions={0} | all-to-all | bytes 1048576 | tf_op jit(solution)/shard_map/while/body/all_to_all | solution.py:289
  432.0 11.9 %all_to_all.71 = bf16[16,8,2048]{2,1,0:T(8,128)(2,1)S(1)} all-to-all(bf16[16,8,2048]{2,1,0:T(8,128)(2,1)S(1)} %broadcast_in_dim.83), channel_id=1, replica_groups=mesh['y'=4,'core'=2,'x'=4,'zh'=2,'zl'=2] {'x','zh','zl'}, dimensions={0} | all-to-all | bytes 1048576 | tf_op jit(solution)/shard_map/while/body/all_to_all | solution.py:28
  454.8 9.6 %all_to_all.73.kv_ref = bf16[8,64,128]{2,1,0:T(8,128)(2,1)S(1)} all-to-all(bf16[8,64,128]{2,1,0:T(8,128)(2,1)S(1)} %broadcast_in_dim.84), channel_id=1, replica_groups=mesh['y'=4,'core'=2,'x'=4,'zh'=2,'zl'=2] {'x','zh'}, dimensions={0} | all-to-all | bytes 262144 | tf_op jit(solution)/shard_map/while/body/all_to_all | solution.py:28
  466.9 13.1 %all_to_all.74 = bf16[16,8,2048]{2,1,0:T(8,128)(2,1)S(1)} all-to-all(bf16[16,8,2048]{2,1,0:T(8,128)(2,1)S(1)} %bitcast.76), channel_id=1, replica_groups=mesh['y'=4,'core'=2,'x'=4,'zh'=2,'zl'=2] {'x','zh','zl'}, dimensions={0} | all-to-all | bytes 1048576 | tf_op jit(solution)/shard_map/while/body/all_to_all | solution.py:289
  480.8 12.0 %all_to_all.71 = bf16[16,8,2048]{2,1,0:T(8,128)(2,1)S(1)} all-to-all(bf16[16,8,2048]{2,1,0:T(8,128)(2,1)S(1)} %broadcast_in_dim.83), channel_id=1, replica_groups=mesh['y'=4,'core'=2,'x'=4,'zh'=2,'zl'=2] {'x','zh','zl'}, dimensions={0} | all-to-all | bytes 1048576 | tf_op jit(solution)/shard_map/while/body/all_to_all | solution.py:28
  503.6 9.7 %all_to_all.73.kv_ref = bf16[8,64,128]{2,1,0:T(8,128)(2,1)S(1)} all-to-all(bf16[8,64,128]{2,1,0:T(8,128)(2,1)S(1)} %broadcast_in_dim.84), channel_id=1, replica_groups=mesh['y'=4,'core'=2,'x'=4,'zh'=2,'zl'=2] {'x','zh'}, dimensions={0} | all-to-all | bytes 262144 | tf_op jit(solution)/shard_map/while/body/all_to_all | solution.py:28
  515.9 11.6 %all_to_all.74 = bf16[16,8,2048]{2,1,0:T(8,128)(2,1)S(1)} all-to-all(bf16[16,8,2048]{2,1,0:T(8,128)(2,1)S(1)} %bitcast.76), channel_id=1, replica_groups=mesh['y'=4,'core'=2,'x'=4,'zh'=2,'zl'=2] {'x','zh','zl'}, dimensions={0} | all-to-all | bytes 1048576 | tf_op jit(solution)/shard_map/while/body/all_to_all | solution.py:289
  530.0 46.6 %all-to-all-start.11 = ((bf16[8,2,1152]{2,1,0:T(2,128)(2,1)}), bf16[8,2,1152]{2,1,0:T(2,128)(2,1)S(1)}, u32[]{:S(2)}, u32[]{:S(2)}) async-start(bf16[8,2,1152]{2,1,0:T(2,128)(2,1)} %reshape.276), calls=%async_computation.11 | async-start | bytes 73728 | tf_op jit(solution)/shard_map/all_to_all | solution.py:317
  (226 shorter events, 259.0 us)
Async XLA Ops:
  2.9 36.4 %collective-permute-start.7 = (bf16[64,8192]{1,0:T(8,128)(2,1)}, bf16[64,8192]{1,0:T(8,128)(2,1)}, u32[]{:S(2)}, u32[]{:S(2)}) collective-permute-start(bf16[64,8192]{1,0:T(8,128)(2,1)} %pad_maximum_fusion), channel_id=1, source_target_pairs={{0,2},{1,0},{2,6},{3,4},{4,10},{5,8},{6,14},{7,12},{8,3},{9,1},{10... | collective-permute-start | bytes 3145736 | tf_op jit(solution)/shard_map/ppermute | solution.py:231
  11.1 38.2 %collective-permute-start.2 = (bf16[2048,256]{1,0:T(8,128)(2,1)S(1)}, bf16[2048,256]{1,0:T(8,128)(2,1)S(1)}, u32[]{:S(2)}, u32[]{:S(2)}) collective-permute-start(bf16[2048,256]{1,0:T(8,128)(2,1)S(1)} %get-tuple-element.467), channel_id=1, source_target_pairs={{0,96},{32,0},{64,32},{96,64},{1,97},{33,1},{65,33},{97,65},{2,98}... | collective-permute-start | bytes 3145736 | tf_op jit(solution)/shard_map/ppermute | solution.py:220
  13.8 54.9 %collective-permute-start.1 = (bf16[2048,256]{1,0:T(8,128)(2,1)}, bf16[2048,256]{1,0:T(8,128)(2,1)}, u32[]{:S(2)}, u32[]{:S(2)}) collective-permute-start(bf16[2048,256]{1,0:T(8,128)(2,1)} %get-tuple-element.468), channel_id=1, source_target_pairs={{0,64},{32,96},{64,0},{96,32},{1,65},{33,97},{65,1},{97,33},{2,66}... | collective-permute-start | bytes 3145736 | tf_op jit(solution)/shard_map/ppermute | solution.py:220
  14.2 57.3 %collective-permute-start = (bf16[2048,256]{1,0:T(8,128)(2,1)}, bf16[2048,256]{1,0:T(8,128)(2,1)}, u32[]{:S(2)}, u32[]{:S(2)}) collective-permute-start(bf16[2048,256]{1,0:T(8,128)(2,1)} %get-tuple-element.469), channel_id=1, source_target_pairs={{0,32},{32,64},{64,96},{96,0},{1,33},{33,65},{65,97},{97,1},{2,34}... | collective-permute-start | bytes 3145736 | tf_op jit(solution)/shard_map/ppermute | solution.py:220
  14.9 59.4 %collective-permute-start.3 = (bf16[2048,256]{1,0:T(8,128)(2,1)S(1)}, bf16[2048,256]{1,0:T(8,128)(2,1)}, u32[]{:S(2)}, u32[]{:S(2)}) collective-permute-start(bf16[2048,256]{1,0:T(8,128)(2,1)S(1)} %get-tuple-element.715.refs_0_), channel_id=1, source_target_pairs={{0,16},{16,0},{1,17},{17,1},{2,18},{18,2},{3,19},{19,3},{4,20},{20... | collective-permute-start | bytes 3145736 | tf_op jit(solution)/shard_map/ppermute | solution.py:223
  23.5 13.0 %all-to-all-start.4 = ((bf16[16,2,8,512]{3,2,1,0:T(8,128)(2,1)}), bf16[16,2,8,512]{3,2,1,0:T(8,128)(2,1)S(1)}, u32[]{:S(2)}, u32[]{:S(2)}) async-start(bf16[16,2,8,512]{3,2,1,0:T(8,128)(2,1)} %fusion.13), calls=%async_computation.4 | async-start | bytes 524288 | tf_op jit(solution)/shard_map/all_to_all | solution.py:251
  41.5 32.8 %collective-permute-start.10 = (bf16[80,2048]{1,0:T(8,128)(2,1)}, bf16[80,2048]{1,0:T(8,128)(2,1)}, u32[]{:S(2)}, u32[]{:S(2)}) collective-permute-start(bf16[80,2048]{1,0:T(8,128)(2,1)} %get-tuple-element.471), channel_id=1, source_target_pairs={{0,96},{32,0},{64,32},{96,64},{1,97},{33,1},{65,33},{97,65},{2,98}... | collective-permute-start | bytes 983048 | tf_op jit(solution)/shard_map/ppermute | solution.py:220
  43.5 24.2 %all-to-all-start.5 = ((bf16[8,8,2048]{2,1,0:T(8,128)(2,1)}), bf16[8,8,2048]{2,1,0:T(8,128)(2,1)}, u32[]{:S(2)}, u32[]{:S(2)}) async-start(bf16[8,8,2048]{2,1,0:T(8,128)(2,1)} %reshape.256), calls=%async_computation.5 | async-start | bytes 524288 | tf_op jit(solution)/shard_map/all_to_all | solution.py:253
  49.3 26.2 %collective-permute-start.8 = (bf16[80,2048]{1,0:T(8,128)(2,1)}, bf16[80,2048]{1,0:T(8,128)(2,1)}, u32[]{:S(2)}, u32[]{:S(2)}) collective-permute-start(bf16[80,2048]{1,0:T(8,128)(2,1)} %get-tuple-element.473), channel_id=1, source_target_pairs={{0,32},{32,64},{64,96},{96,0},{1,33},{33,65},{65,97},{97,1},{2,34}... | collective-permute-start | bytes 983048 | tf_op jit(solution)/shard_map/ppermute | solution.py:220
  68.7 65.8 %collective-permute-start.15 = (bf16[256,2048]{1,0:T(8,128)(2,1)}, bf16[256,2048]{1,0:T(8,128)(2,1)}, u32[]{:S(2)}, u32[]{:S(2)}) collective-permute-start(bf16[256,2048]{1,0:T(8,128)(2,1)} %get-tuple-element.222), channel_id=1, source_target_pairs={{0,32},{32,64},{64,96},{96,0},{1,33},{33,65},{65,97},{97,1},{2,34}... | collective-permute-start | bytes 3145736 | tf_op jit(solution)/shard_map/ppermute | solution.py:220
  71.5 63.9 %collective-permute-start.16 = (bf16[256,2048]{1,0:T(8,128)(2,1)}, bf16[256,2048]{1,0:T(8,128)(2,1)}, u32[]{:S(2)}, u32[]{:S(2)}) collective-permute-start(bf16[256,2048]{1,0:T(8,128)(2,1)} %get-tuple-element.223), channel_id=1, source_target_pairs={{0,64},{32,96},{64,0},{96,32},{1,65},{33,97},{65,1},{97,33},{2,66}... | collective-permute-start | bytes 3145736 | tf_op jit(solution)/shard_map/ppermute | solution.py:220
  74.3 61.2 %collective-permute-start.17 = (bf16[256,2048]{1,0:T(8,128)(2,1)}, bf16[256,2048]{1,0:T(8,128)(2,1)}, u32[]{:S(2)}, u32[]{:S(2)}) collective-permute-start(bf16[256,2048]{1,0:T(8,128)(2,1)} %get-tuple-element.224), channel_id=1, source_target_pairs={{0,96},{32,0},{64,32},{96,64},{1,97},{33,1},{65,33},{97,65},{2,98}... | collective-permute-start | bytes 3145736 | tf_op jit(solution)/shard_map/ppermute | solution.py:220
  74.3 52.0 %collective-permute-start.9 = (bf16[80,2048]{1,0:T(8,128)(2,1)}, bf16[80,2048]{1,0:T(8,128)(2,1)}, u32[]{:S(2)}, u32[]{:S(2)}) collective-permute-start(bf16[80,2048]{1,0:T(8,128)(2,1)} %get-tuple-element.474), channel_id=1, source_target_pairs={{0,64},{32,96},{64,0},{96,32},{1,65},{33,97},{65,1},{97,33},{2,66}... | collective-permute-start | bytes 983048 | tf_op jit(solution)/shard_map/ppermute | solution.py:220
  75.6 52.6 %collective-permute-start.11 = (bf16[80,2048]{1,0:T(8,128)(2,1)S(1)}, bf16[80,2048]{1,0:T(8,128)(2,1)}, u32[]{:S(2)}, u32[]{:S(2)}) collective-permute-start(bf16[80,2048]{1,0:T(8,128)(2,1)S(1)} %get-tuple-element.723.refs_8_), channel_id=1, source_target_pairs={{0,16},{16,0},{1,17},{17,1},{2,18},{18,2},{3,19},{19,3},{4,20},{20... | collective-permute-start | bytes 983048 | tf_op jit(solution)/shard_map/ppermute | solution.py:223
  126.3 13.5 %collective-permute-start.6 = (bf16[2048,256]{1,0:T(8,128)(2,1)S(1)}, bf16[2048,256]{1,0:T(8,128)(2,1)}, u32[]{:S(2)}, u32[]{:S(2)}) collective-permute-start(bf16[2048,256]{1,0:T(8,128)(2,1)S(1)} %collective-permute-done.2.refs_3_), channel_id=1, source_target_pairs={{0,16},{16,0},{1,17},{17,1},{2,18},{18,2},{3,19},{19,3},{4,20},{20... | collective-permute-start | bytes 3145736 | tf_op jit(solution)/shard_map/ppermute | solution.py:223
  128.2 11.8 %collective-permute-start.5 = (bf16[2048,256]{1,0:T(8,128)(2,1)}, bf16[2048,256]{1,0:T(8,128)(2,1)}, u32[]{:S(2)}, u32[]{:S(2)}) collective-permute-start(bf16[2048,256]{1,0:T(8,128)(2,1)} %collective-permute-done.1.refs_2_), channel_id=1, source_target_pairs={{0,16},{16,0},{1,17},{17,1},{2,18},{18,2},{3,19},{19,3},{4,20},{20... | collective-permute-start | bytes 3145736 | tf_op jit(solution)/shard_map/ppermute | solution.py:223
  129.3 20.9 %all-to-all-start.6 = ((bf16[16,12,2048]{2,1,0:T(8,128)(2,1)}), bf16[16,12,2048]{2,1,0:T(8,128)(2,1)}, u32[]{:S(2)}, u32[]{:S(2)}) async-start(bf16[16,12,2048]{2,1,0:T(8,128)(2,1)} %broadcast_in_dim.75), calls=%async_computation.6 | async-start | bytes 2097152 | tf_op jit(solution)/shard_map/all_to_all | solution.py:28
  135.4 15.9 %collective-permute-start.4 = (bf16[2048,256]{1,0:T(8,128)(2,1)}, bf16[2048,256]{1,0:T(8,128)(2,1)}, u32[]{:S(2)}, u32[]{:S(2)}) collective-permute-start(bf16[2048,256]{1,0:T(8,128)(2,1)} %collective-permute-done.refs_1_), channel_id=1, source_target_pairs={{0,16},{16,0},{1,17},{17,1},{2,18},{18,2},{3,19},{19,3},{4,20},{20... | collective-permute-start | bytes 3145736 | tf_op jit(solution)/shard_map/ppermute | solution.py:223
  139.0 32.3 %collective-permute-start.18 = (bf16[256,2048]{1,0:T(8,128)(2,1)S(1)}, bf16[256,2048]{1,0:T(8,128)(2,1)}, u32[]{:S(2)}, u32[]{:S(2)}) collective-permute-start(bf16[256,2048]{1,0:T(8,128)(2,1)S(1)} %get-tuple-element.735.refs_0_), channel_id=1, source_target_pairs={{0,16},{16,0},{1,17},{17,1},{2,18},{18,2},{3,19},{19,3},{4,20},{20... | collective-permute-start | bytes 3145736 | tf_op jit(solution)/shard_map/ppermute | solution.py:223
  139.4 36.1 %collective-permute-start.19 = (bf16[256,2048]{1,0:T(8,128)(2,1)}, bf16[256,2048]{1,0:T(8,128)(2,1)}, u32[]{:S(2)}, u32[]{:S(2)}) collective-permute-start(bf16[256,2048]{1,0:T(8,128)(2,1)} %collective-permute-done.15.refs_1_), channel_id=1, source_target_pairs={{0,16},{16,0},{1,17},{17,1},{2,18},{18,2},{3,19},{19,3},{4,20},{20... | collective-permute-start | bytes 3145736 | tf_op jit(solution)/shard_map/ppermute | solution.py:223
  139.8 35.7 %collective-permute-start.20 = (bf16[256,2048]{1,0:T(8,128)(2,1)}, bf16[256,2048]{1,0:T(8,128)(2,1)}, u32[]{:S(2)}, u32[]{:S(2)}) collective-permute-start(bf16[256,2048]{1,0:T(8,128)(2,1)} %collective-permute-done.16.refs_2_), channel_id=1, source_target_pairs={{0,16},{16,0},{1,17},{17,1},{2,18},{18,2},{3,19},{19,3},{4,20},{20... | collective-permute-start | bytes 3145736 | tf_op jit(solution)/shard_map/ppermute | solution.py:223
  140.0 35.6 %collective-permute-start.21 = (bf16[256,2048]{1,0:T(8,128)(2,1)}, bf16[256,2048]{1,0:T(8,128)(2,1)}, u32[]{:S(2)}, u32[]{:S(2)}) collective-permute-start(bf16[256,2048]{1,0:T(8,128)(2,1)} %collective-permute-done.17.refs_3_), channel_id=1, source_target_pairs={{0,16},{16,0},{1,17},{17,1},{2,18},{18,2},{3,19},{19,3},{4,20},{20... | collective-permute-start | bytes 3145736 | tf_op jit(solution)/shard_map/ppermute | solution.py:223
  178.9 12.6 %all-to-all-start.9 = ((bf16[16,8,2048]{2,1,0:T(8,128)(2,1)}), bf16[16,8,2048]{2,1,0:T(8,128)(2,1)S(1)}, u32[]{:S(2)}, u32[]{:S(2)}) async-start(bf16[16,8,2048]{2,1,0:T(8,128)(2,1)} %bitcast.30), calls=%async_computation.9 | async-start | bytes 1048576 | tf_op jit(solution)/shard_map/all_to_all | solution.py:289
  530.0 51.3 %all-to-all-start.11 = ((bf16[8,2,1152]{2,1,0:T(2,128)(2,1)}), bf16[8,2,1152]{2,1,0:T(2,128)(2,1)S(1)}, u32[]{:S(2)}, u32[]{:S(2)}) async-start(bf16[8,2,1152]{2,1,0:T(2,128)(2,1)} %reshape.276), calls=%async_computation.11 | async-start | bytes 73728 | tf_op jit(solution)/shard_map/all_to_all | solution.py:317
  (15 other events, 256.2 us)

commit v2 on v1

--- a/solution.py
+++ b/solution.py
@@ -64,7 +64,11 @@
     out_ref, q_buf, kv_buf, sems = refs[2 * count :]
     choice = choice_of(state_ref)
     fetch(choice, kv_refs, kv_buf, sems.at[0])
-    fetch(choice, q_refs, q_buf, sems.at[1])
+    half = q_buf.shape[0] // 2
+    tops = [ref.at[pl.ds(0, half), :] for ref in q_refs]
+    ends = [ref.at[pl.ds(half, half), :] for ref in q_refs]
+    fetch(choice, tops, q_buf.at[pl.ds(0, half), :], sems.at[1])
+    fetch(choice, ends, q_buf.at[pl.ds(half, half), :], sems.at[2])
     values = x_ref[...].astype(jnp.float32)
     length, _ = values.shape
     square = jnp.sum(values * values, axis=1, keepdims=True)
@@ -79,8 +83,11 @@
     kv_part = lax.dot_general(
         kv_buf[:rows, :], lhs, (((1,), (1,)), ((), ())), preferred_element_type=jnp.float32
     ).astype(jnp.bfloat16)
-    pltpu.make_async_copy(q_refs[0], q_buf, sems.at[1]).wait()
-    query = jnp.dot(lhs, q_buf[...], preferred_element_type=jnp.float32).astype(jnp.bfloat16)
+    pltpu.make_async_copy(tops[0], q_buf.at[pl.ds(0, half), :], sems.at[1]).wait()
+    query = jnp.dot(lhs[:, :half], q_buf[:half, :], preferred_element_type=jnp.float32)
+    pltpu.make_async_copy(ends[0], q_buf.at[pl.ds(half, half), :], sems.at[2]).wait()
+    query += jnp.dot(lhs[:, half:], q_buf[half:, :], preferred_element_type=jnp.float32)
+    query = query.astype(jnp.bfloat16)
     heads = query.shape[1] // HEAD_DIM
     for copy in range(N_Y):
         for h in range(heads):
@@ -161,7 +168,7 @@
         scratch_shapes=[
             pltpu.VMEM(blocks_q[0].shape, jnp.bfloat16),
             pltpu.VMEM(blocks_kv[0].shape, jnp.bfloat16),
-            pltpu.SemaphoreType.DMA((2,)),
+            pltpu.SemaphoreType.DMA((3,)),
         ],
         compiler_params=pltpu.CompilerParams(vmem_limit_bytes=16 << 20),
         name="front",
@@ -254,7 +261,7 @@
     resid = jnp.sum(found.astype(f32), axis=0).astype(bf16)
 
     blocks_out = spread(
-        lambda block: lax.dynamic_slice_in_dim(w_out[0], block * part, part, axis=1), resid
+        lambda block: lax.dynamic_slice_in_dim(w_out[0], block * part, part, axis=1),
     )
 
     seen_q, seen_k, seen_v, seen_out, _ = lax.optimization_barrier(

time: 596 us -> 578 us (0.970)
  waiting for transfers between devices: 95.9 us -> 33.4 us
  starting transfers between devices: 105 us -> 153 us
    ppermute x12, starting transfers between devices: 8.58 us -> 62.3 us  [spread(): twins.append(lax.ppermute(own[step], 'core', swap))]
    ppermute x9, waiting for transfers between devices: 45.2 us -> 7.16 us  [spread(): own[step] = lax.ppermute(own[step], 'y', turn)]
    all_to_all x1, waiting for transfers between devices: 12.9 us -> 0.37 us  [program(): lax.all_to_all(came.reshape(layers, own_rows, part), SECTION, 0, 0, tiled...]
    all_to_all x1, waiting for transfers between devices: 6.94 us -> 0.01 us  [program(): came = lax.all_to_all(sent, TP, 0, 0, tiled=True)]
  transfers between devices with their start and end apart: 30 -> 30, of which waited for: 11 -> 12; matrix products, arithmetic and copies ran while one was open for 7% -> 7% of each run, Pallas kernels for 1% -> 1%
where the time goes in v2:
time: 578 us; the launch traced here: 576 us
  blocking collectives  295 us (51%)
  starting transfers between devices  153 us (26%)
  Pallas kernels  40.1 us (7%)
  waiting for transfers between devices  33.4 us (6%)
  local copies, waits for them, and re-layouts  27.9 us (5%)
  other arithmetic  24 us (4%)
    all_to_all x14, blocking collectives, copy_for_each(): lax.all_to_all(jnp.broadcast_to(value[None], (count, *value.shape)), axis...  154 us
    all_to_all x7, blocking collectives, one_layer(): lax.all_to_all(head_part.reshape(N_TP, own_rows, part), TP, 0, 0, tiled=T...  81.7 us
    ppermute x12, starting transfers between devices, spread(): twins.append(lax.ppermute(own[step], 'core', swap))  62.3 us
    all_to_all x7, blocking collectives, one_layer(): packed = lax.all_to_all(packed, 'y', 0, 0, tiled=True)  59 us
    all_to_all x1, starting transfers between devices, program(): lax.all_to_all(peaks.astype(bf16), SECTION, 0, 0, tiled=True).astype(f32)  45 us
    pallas_call x8, Pallas kernels, back(): pl.pallas_call(back_body, out_shape=(jax.ShapeDtypeStruct((length, part),...  20.3 us
    pallas_call x8, Pallas kernels, front(): pl.pallas_call(front_body, out_shape=jax.ShapeDtypeStruct((N_Y, rows, len...  19.8 us
    ppermute x9, starting transfers between devices, spread(): own[step] = lax.ppermute(own[step], 'y', turn)  12.8 us
  transfers between devices with their start and end apart: 30, of which 12 were waited for; matrix products, arithmetic and copies ran while one was open for 7% of the time, Pallas kernels for 1%

profile of v2, /device:TPU:1, one launch (start us, length us, event | category | flops | bytes accessed | tf_op | source)
XLA Modules:
  0.0 575.6 jit_solution(8296553329406361924)
XLA Ops:
  40.3 46.9 %collective-permute-start.3 = (bf16[2048,256]{1,0:T(8,128)(2,1)S(1)}, bf16[2048,256]{1,0:T(8,128)(2,1)}, u32[]{:S(2)}, u32[]{:S(2)}) collective-permute-start(bf16[2048,256]{1,0:T(8,128)(2,1)S(1)} %get-tuple-element.707.refs_0_), channel_id=1, source_target_pairs={{0,16},{16,0},{1,17},{17,1},{2,18},{18,2},{3,19},{19,3},{4,20},{20... | collective-permute-start | bytes 3145736 | tf_op jit(solution)/shard_map/ppermute | solution.py:230
  177.2 334.9 %while.16 = (u32[]{:T(128)}, bf16[8,2048]{1,0:T(8,128)(2,1)S(1)}, bf16[8,8,2048]{2,1,0:T(8,128)(2,1)}, bf16[8,2304]{1,0:T(8,128)(2,1)S(1)}, s32[3]{0:T(128)S(1)}...) while((u32[]{:T(128)}, bf16[8,2048]{1,0:T(8,128)(2,1)S(1)}, ...), condition=%wide.region_9.10_spmd, body=%wide.region_6.9_spmd.sunk | while | flops 874892 | bytes 5124449 | solution.py:322
  177.2 12.2 %all_to_all.71 = bf16[16,8,2048]{2,1,0:T(8,128)(2,1)S(1)} all-to-all(bf16[16,8,2048]{2,1,0:T(8,128)(2,1)S(1)} %broadcast_in_dim.83), channel_id=1, replica_groups=mesh['y'=4,'core'=2,'x'=4,'zh'=2,'zl'=2] {'x','zh','zl'}, dimensions={0} | all-to-all | bytes 1048576 | tf_op jit(solution)/shard_map/while/body/all_to_all | solution.py:28
  199.8 9.6 %all_to_all.73.kv_ref = bf16[8,64,128]{2,1,0:T(8,128)(2,1)S(1)} all-to-all(bf16[8,64,128]{2,1,0:T(8,128)(2,1)S(1)} %broadcast_in_dim.84), channel_id=1, replica_groups=mesh['y'=4,'core'=2,'x'=4,'zh'=2,'zl'=2] {'x','zh'}, dimensions={0} | all-to-all | bytes 262144 | tf_op jit(solution)/shard_map/while/body/all_to_all | solution.py:28
  211.3 11.6 %all_to_all.74 = bf16[16,8,2048]{2,1,0:T(8,128)(2,1)S(1)} all-to-all(bf16[16,8,2048]{2,1,0:T(8,128)(2,1)S(1)} %bitcast.76), channel_id=1, replica_groups=mesh['y'=4,'core'=2,'x'=4,'zh'=2,'zl'=2] {'x','zh','zl'}, dimensions={0} | all-to-all | bytes 1048576 | tf_op jit(solution)/shard_map/while/body/all_to_all | solution.py:296
  223.7 12.7 %all_to_all.71 = bf16[16,8,2048]{2,1,0:T(8,128)(2,1)S(1)} all-to-all(bf16[16,8,2048]{2,1,0:T(8,128)(2,1)S(1)} %broadcast_in_dim.83), channel_id=1, replica_groups=mesh['y'=4,'core'=2,'x'=4,'zh'=2,'zl'=2] {'x','zh','zl'}, dimensions={0} | all-to-all | bytes 1048576 | tf_op jit(solution)/shard_map/while/body/all_to_all | solution.py:28
  247.7 9.3 %all_to_all.73.kv_ref = bf16[8,64,128]{2,1,0:T(8,128)(2,1)S(1)} all-to-all(bf16[8,64,128]{2,1,0:T(8,128)(2,1)S(1)} %broadcast_in_dim.84), channel_id=1, replica_groups=mesh['y'=4,'core'=2,'x'=4,'zh'=2,'zl'=2] {'x','zh'}, dimensions={0} | all-to-all | bytes 262144 | tf_op jit(solution)/shard_map/while/body/all_to_all | solution.py:28
  259.5 11.6 %all_to_all.74 = bf16[16,8,2048]{2,1,0:T(8,128)(2,1)S(1)} all-to-all(bf16[16,8,2048]{2,1,0:T(8,128)(2,1)S(1)} %bitcast.76), channel_id=1, replica_groups=mesh['y'=4,'core'=2,'x'=4,'zh'=2,'zl'=2] {'x','zh','zl'}, dimensions={0} | all-to-all | bytes 1048576 | tf_op jit(solution)/shard_map/while/body/all_to_all | solution.py:296
  271.9 12.6 %all_to_all.71 = bf16[16,8,2048]{2,1,0:T(8,128)(2,1)S(1)} all-to-all(bf16[16,8,2048]{2,1,0:T(8,128)(2,1)S(1)} %broadcast_in_dim.83), channel_id=1, replica_groups=mesh['y'=4,'core'=2,'x'=4,'zh'=2,'zl'=2] {'x','zh','zl'}, dimensions={0} | all-to-all | bytes 1048576 | tf_op jit(solution)/shard_map/while/body/all_to_all | solution.py:28
  295.4 9.6 %all_to_all.73.kv_ref = bf16[8,64,128]{2,1,0:T(8,128)(2,1)S(1)} all-to-all(bf16[8,64,128]{2,1,0:T(8,128)(2,1)S(1)} %broadcast_in_dim.84), channel_id=1, replica_groups=mesh['y'=4,'core'=2,'x'=4,'zh'=2,'zl'=2] {'x','zh'}, dimensions={0} | all-to-all | bytes 262144 | tf_op jit(solution)/shard_map/while/body/all_to_all | solution.py:28
  307.6 11.6 %all_to_all.74 = bf16[16,8,2048]{2,1,0:T(8,128)(2,1)S(1)} all-to-all(bf16[16,8,2048]{2,1,0:T(8,128)(2,1)S(1)} %bitcast.76), channel_id=1, replica_groups=mesh['y'=4,'core'=2,'x'=4,'zh'=2,'zl'=2] {'x','zh','zl'}, dimensions={0} | all-to-all | bytes 1048576 | tf_op jit(solution)/shard_map/while/body/all_to_all | solution.py:296
  320.0 11.9 %all_to_all.71 = bf16[16,8,2048]{2,1,0:T(8,128)(2,1)S(1)} all-to-all(bf16[16,8,2048]{2,1,0:T(8,128)(2,1)S(1)} %broadcast_in_dim.83), channel_id=1, replica_groups=mesh['y'=4,'core'=2,'x'=4,'zh'=2,'zl'=2] {'x','zh','zl'}, dimensions={0} | all-to-all | bytes 1048576 | tf_op jit(solution)/shard_map/while/body/all_to_all | solution.py:28
  342.8 11.0 %all_to_all.73.kv_ref = bf16[8,64,128]{2,1,0:T(8,128)(2,1)S(1)} all-to-all(bf16[8,64,128]{2,1,0:T(8,128)(2,1)S(1)} %broadcast_in_dim.84), channel_id=1, replica_groups=mesh['y'=4,'core'=2,'x'=4,'zh'=2,'zl'=2] {'x','zh'}, dimensions={0} | all-to-all | bytes 262144 | tf_op jit(solution)/shard_map/while/body/all_to_all | solution.py:28
  356.4 11.6 %all_to_all.74 = bf16[16,8,2048]{2,1,0:T(8,128)(2,1)S(1)} all-to-all(bf16[16,8,2048]{2,1,0:T(8,128)(2,1)S(1)} %bitcast.76), channel_id=1, replica_groups=mesh['y'=4,'core'=2,'x'=4,'zh'=2,'zl'=2] {'x','zh','zl'}, dimensions={0} | all-to-all | bytes 1048576 | tf_op jit(solution)/shard_map/while/body/all_to_all | solution.py:296
  368.8 12.2 %all_to_all.71 = bf16[16,8,2048]{2,1,0:T(8,128)(2,1)S(1)} all-to-all(bf16[16,8,2048]{2,1,0:T(8,128)(2,1)S(1)} %broadcast_in_dim.83), channel_id=1, replica_groups=mesh['y'=4,'core'=2,'x'=4,'zh'=2,'zl'=2] {'x','zh','zl'}, dimensions={0} | all-to-all | bytes 1048576 | tf_op jit(solution)/shard_map/while/body/all_to_all | solution.py:28
  392.2 9.2 %all_to_all.73.kv_ref = bf16[8,64,128]{2,1,0:T(8,128)(2,1)S(1)} all-to-all(bf16[8,64,128]{2,1,0:T(8,128)(2,1)S(1)} %broadcast_in_dim.84), channel_id=1, replica_groups=mesh['y'=4,'core'=2,'x'=4,'zh'=2,'zl'=2] {'x','zh'}, dimensions={0} | all-to-all | bytes 262144 | tf_op jit(solution)/shard_map/while/body/all_to_all | solution.py:28
  403.9 11.6 %all_to_all.74 = bf16[16,8,2048]{2,1,0:T(8,128)(2,1)S(1)} all-to-all(bf16[16,8,2048]{2,1,0:T(8,128)(2,1)S(1)} %bitcast.76), channel_id=1, replica_groups=mesh['y'=4,'core'=2,'x'=4,'zh'=2,'zl'=2] {'x','zh','zl'}, dimensions={0} | all-to-all | bytes 1048576 | tf_op jit(solution)/shard_map/while/body/all_to_all | solution.py:296
  416.3 11.9 %all_to_all.71 = bf16[16,8,2048]{2,1,0:T(8,128)(2,1)S(1)} all-to-all(bf16[16,8,2048]{2,1,0:T(8,128)(2,1)S(1)} %broadcast_in_dim.83), channel_id=1, replica_groups=mesh['y'=4,'core'=2,'x'=4,'zh'=2,'zl'=2] {'x','zh','zl'}, dimensions={0} | all-to-all | bytes 1048576 | tf_op jit(solution)/shard_map/while/body/all_to_all | solution.py:28
  439.1 9.6 %all_to_all.73.kv_ref = bf16[8,64,128]{2,1,0:T(8,128)(2,1)S(1)} all-to-all(bf16[8,64,128]{2,1,0:T(8,128)(2,1)S(1)} %broadcast_in_dim.84), channel_id=1, replica_groups=mesh['y'=4,'core'=2,'x'=4,'zh'=2,'zl'=2] {'x','zh'}, dimensions={0} | all-to-all | bytes 262144 | tf_op jit(solution)/shard_map/while/body/all_to_all | solution.py:28
  451.3 12.1 %all_to_all.74 = bf16[16,8,2048]{2,1,0:T(8,128)(2,1)S(1)} all-to-all(bf16[16,8,2048]{2,1,0:T(8,128)(2,1)S(1)} %bitcast.76), channel_id=1, replica_groups=mesh['y'=4,'core'=2,'x'=4,'zh'=2,'zl'=2] {'x','zh','zl'}, dimensions={0} | all-to-all | bytes 1048576 | tf_op jit(solution)/shard_map/while/body/all_to_all | solution.py:296
  464.2 11.9 %all_to_all.71 = bf16[16,8,2048]{2,1,0:T(8,128)(2,1)S(1)} all-to-all(bf16[16,8,2048]{2,1,0:T(8,128)(2,1)S(1)} %broadcast_in_dim.83), channel_id=1, replica_groups=mesh['y'=4,'core'=2,'x'=4,'zh'=2,'zl'=2] {'x','zh','zl'}, dimensions={0} | all-to-all | bytes 1048576 | tf_op jit(solution)/shard_map/while/body/all_to_all | solution.py:28
  487.1 9.9 %all_to_all.73.kv_ref = bf16[8,64,128]{2,1,0:T(8,128)(2,1)S(1)} all-to-all(bf16[8,64,128]{2,1,0:T(8,128)(2,1)S(1)} %broadcast_in_dim.84), channel_id=1, replica_groups=mesh['y'=4,'core'=2,'x'=4,'zh'=2,'zl'=2] {'x','zh'}, dimensions={0} | all-to-all | bytes 262144 | tf_op jit(solution)/shard_map/while/body/all_to_all | solution.py:28
  499.5 11.8 %all_to_all.74 = bf16[16,8,2048]{2,1,0:T(8,128)(2,1)S(1)} all-to-all(bf16[16,8,2048]{2,1,0:T(8,128)(2,1)S(1)} %bitcast.76), channel_id=1, replica_groups=mesh['y'=4,'core'=2,'x'=4,'zh'=2,'zl'=2] {'x','zh','zl'}, dimensions={0} | all-to-all | bytes 1048576 | tf_op jit(solution)/shard_map/while/body/all_to_all | solution.py:296
  513.9 45.0 %all-to-all-start.11 = ((bf16[8,2,1152]{2,1,0:T(2,128)(2,1)}), bf16[8,2,1152]{2,1,0:T(2,128)(2,1)S(1)}, u32[]{:S(2)}, u32[]{:S(2)}) async-start(bf16[8,2,1152]{2,1,0:T(2,128)(2,1)} %reshape.276), calls=%async_computation.11 | async-start | bytes 73728 | tf_op jit(solution)/shard_map/all_to_all | solution.py:324
  (226 shorter events, 245.8 us)
Async XLA Ops:
  2.9 28.0 %collective-permute-start.7 = (bf16[64,8192]{1,0:T(8,128)(2,1)}, bf16[64,8192]{1,0:T(8,128)(2,1)}, u32[]{:S(2)}, u32[]{:S(2)}) collective-permute-start(bf16[64,8192]{1,0:T(8,128)(2,1)} %pad_maximum_fusion), channel_id=1, source_target_pairs={{0,2},{1,0},{2,6},{3,4},{4,10},{5,8},{6,14},{7,12},{8,3},{9,1},{10... | collective-permute-start | bytes 3145736 | tf_op jit(solution)/shard_map/ppermute | solution.py:238
  11.6 25.7 %collective-permute-start.17 = (bf16[256,2048]{1,0:T(8,128)(2,1)}, bf16[256,2048]{1,0:T(8,128)(2,1)}, u32[]{:S(2)}, u32[]{:S(2)}) collective-permute-start(bf16[256,2048]{1,0:T(8,128)(2,1)} %get-tuple-element.455), channel_id=1, source_target_pairs={{0,96},{32,0},{64,32},{96,64},{1,97},{33,1},{65,33},{97,65},{2,98}... | collective-permute-start | bytes 3145736 | tf_op jit(solution)/shard_map/ppermute | solution.py:227
  14.3 26.0 %collective-permute-start.15 = (bf16[256,2048]{1,0:T(8,128)(2,1)}, bf16[256,2048]{1,0:T(8,128)(2,1)}, u32[]{:S(2)}, u32[]{:S(2)}) collective-permute-start(bf16[256,2048]{1,0:T(8,128)(2,1)} %get-tuple-element.456), channel_id=1, source_target_pairs={{0,32},{32,64},{64,96},{96,0},{1,33},{33,65},{65,97},{97,1},{2,34}... | collective-permute-start | bytes 3145736 | tf_op jit(solution)/shard_map/ppermute | solution.py:227
  14.3 86.0 %collective-permute-start.16 = (bf16[256,2048]{1,0:T(8,128)(2,1)}, bf16[256,2048]{1,0:T(8,128)(2,1)}, u32[]{:S(2)}, u32[]{:S(2)}) collective-permute-start(bf16[256,2048]{1,0:T(8,128)(2,1)} %get-tuple-element.458), channel_id=1, source_target_pairs={{0,64},{32,96},{64,0},{96,32},{1,65},{33,97},{65,1},{97,33},{2,66}... | collective-permute-start | bytes 3145736 | tf_op jit(solution)/shard_map/ppermute | solution.py:227
  17.7 85.1 %collective-permute-start.2 = (bf16[2048,256]{1,0:T(8,128)(2,1)}, bf16[2048,256]{1,0:T(8,128)(2,1)}, u32[]{:S(2)}, u32[]{:S(2)}) collective-permute-start(bf16[2048,256]{1,0:T(8,128)(2,1)} %get-tuple-element.459), channel_id=1, source_target_pairs={{0,96},{32,0},{64,32},{96,64},{1,97},{33,1},{65,33},{97,65},{2,98}... | collective-permute-start | bytes 3145736 | tf_op jit(solution)/shard_map/ppermute | solution.py:227
  25.6 61.8 %all-to-all-start.4 = ((bf16[16,2,8,512]{3,2,1,0:T(8,128)(2,1)}), bf16[16,2,8,512]{3,2,1,0:T(8,128)(2,1)}, u32[]{:S(2)}, u32[]{:S(2)}) async-start(bf16[16,2,8,512]{3,2,1,0:T(8,128)(2,1)} %fusion.13), calls=%async_computation.4 | async-start | bytes 524288 | tf_op jit(solution)/shard_map/all_to_all | solution.py:258
  30.9 71.9 %collective-permute-start.1 = (bf16[2048,256]{1,0:T(8,128)(2,1)}, bf16[2048,256]{1,0:T(8,128)(2,1)}, u32[]{:S(2)}, u32[]{:S(2)}) collective-permute-start(bf16[2048,256]{1,0:T(8,128)(2,1)} %get-tuple-element.460), channel_id=1, source_target_pairs={{0,64},{32,96},{64,0},{96,32},{1,65},{33,97},{65,1},{97,33},{2,66}... | collective-permute-start | bytes 3145736 | tf_op jit(solution)/shard_map/ppermute | solution.py:227
  37.2 70.6 %collective-permute-start = (bf16[2048,256]{1,0:T(8,128)(2,1)}, bf16[2048,256]{1,0:T(8,128)(2,1)}, u32[]{:S(2)}, u32[]{:S(2)}) collective-permute-start(bf16[2048,256]{1,0:T(8,128)(2,1)} %get-tuple-element.461), channel_id=1, source_target_pairs={{0,32},{32,64},{64,96},{96,0},{1,33},{33,65},{65,97},{97,1},{2,34}... | collective-permute-start | bytes 3145736 | tf_op jit(solution)/shard_map/ppermute | solution.py:227
  40.3 70.6 %collective-permute-start.3 = (bf16[2048,256]{1,0:T(8,128)(2,1)S(1)}, bf16[2048,256]{1,0:T(8,128)(2,1)}, u32[]{:S(2)}, u32[]{:S(2)}) collective-permute-start(bf16[2048,256]{1,0:T(8,128)(2,1)S(1)} %get-tuple-element.707.refs_0_), channel_id=1, source_target_pairs={{0,16},{16,0},{1,17},{17,1},{2,18},{18,2},{3,19},{19,3},{4,20},{20... | collective-permute-start | bytes 3145736 | tf_op jit(solution)/shard_map/ppermute | solution.py:230
  94.7 16.1 %all-to-all-start.5 = ((bf16[8,8,2048]{2,1,0:T(8,128)(2,1)}), bf16[8,8,2048]{2,1,0:T(8,128)(2,1)S(1)}, u32[]{:S(2)}, u32[]{:S(2)}) async-start(bf16[8,8,2048]{2,1,0:T(8,128)(2,1)} %reshape.256), calls=%async_computation.5 | async-start | bytes 524288 | tf_op jit(solution)/shard_map/all_to_all | solution.py:260
  100.3 19.4 %collective-permute-start.10 = (bf16[80,2048]{1,0:T(8,128)(2,1)}, bf16[80,2048]{1,0:T(8,128)(2,1)}, u32[]{:S(2)}, u32[]{:S(2)}) collective-permute-start(bf16[80,2048]{1,0:T(8,128)(2,1)} %get-tuple-element.463), channel_id=1, source_target_pairs={{0,96},{32,0},{64,32},{96,64},{1,97},{33,1},{65,33},{97,65},{2,98}... | collective-permute-start | bytes 983048 | tf_op jit(solution)/shard_map/ppermute | solution.py:227
  102.8 19.5 %collective-permute-start.8 = (bf16[80,2048]{1,0:T(8,128)(2,1)}, bf16[80,2048]{1,0:T(8,128)(2,1)}, u32[]{:S(2)}, u32[]{:S(2)}) collective-permute-start(bf16[80,2048]{1,0:T(8,128)(2,1)} %get-tuple-element.465), channel_id=1, source_target_pairs={{0,32},{32,64},{64,96},{96,0},{1,33},{33,65},{65,97},{97,1},{2,34}... | collective-permute-start | bytes 983048 | tf_op jit(solution)/shard_map/ppermute | solution.py:227
  102.8 26.9 %collective-permute-start.6 = (bf16[2048,256]{1,0:T(8,128)(2,1)}, bf16[2048,256]{1,0:T(8,128)(2,1)}, u32[]{:S(2)}, u32[]{:S(2)}) collective-permute-start(bf16[2048,256]{1,0:T(8,128)(2,1)} %collective-permute-done.2.refs_3_), channel_id=1, source_target_pairs={{0,16},{16,0},{1,17},{17,1},{2,18},{18,2},{3,19},{19,3},{4,20},{20... | collective-permute-start | bytes 3145736 | tf_op jit(solution)/shard_map/ppermute | solution.py:230
  107.8 22.0 %collective-permute-start.5 = (bf16[2048,256]{1,0:T(8,128)(2,1)}, bf16[2048,256]{1,0:T(8,128)(2,1)}, u32[]{:S(2)}, u32[]{:S(2)}) collective-permute-start(bf16[2048,256]{1,0:T(8,128)(2,1)} %collective-permute-done.1.refs_2_), channel_id=1, source_target_pairs={{0,16},{16,0},{1,17},{17,1},{2,18},{18,2},{3,19},{19,3},{4,20},{20... | collective-permute-start | bytes 3145736 | tf_op jit(solution)/shard_map/ppermute | solution.py:230
  110.9 11.4 %collective-permute-start.9 = (bf16[80,2048]{1,0:T(8,128)(2,1)S(1)}, bf16[80,2048]{1,0:T(8,128)(2,1)}, u32[]{:S(2)}, u32[]{:S(2)}) collective-permute-start(bf16[80,2048]{1,0:T(8,128)(2,1)S(1)} %get-tuple-element.466), channel_id=1, source_target_pairs={{0,64},{32,96},{64,0},{96,32},{1,65},{33,97},{65,1},{97,33},{2,66}... | collective-permute-start | bytes 983048 | tf_op jit(solution)/shard_map/ppermute | solution.py:227
  114.5 20.9 %all-to-all-start.6 = ((bf16[16,12,2048]{2,1,0:T(8,128)(2,1)}), bf16[16,12,2048]{2,1,0:T(8,128)(2,1)}, u32[]{:S(2)}, u32[]{:S(2)}) async-start(bf16[16,12,2048]{2,1,0:T(8,128)(2,1)} %broadcast_in_dim.75), calls=%async_computation.6 | async-start | bytes 2097152 | tf_op jit(solution)/shard_map/all_to_all | solution.py:28
  122.3 14.2 %collective-permute-start.4 = (bf16[2048,256]{1,0:T(8,128)(2,1)}, bf16[2048,256]{1,0:T(8,128)(2,1)}, u32[]{:S(2)}, u32[]{:S(2)}) collective-permute-start(bf16[2048,256]{1,0:T(8,128)(2,1)} %collective-permute-done.refs_1_), channel_id=1, source_target_pairs={{0,16},{16,0},{1,17},{17,1},{2,18},{18,2},{3,19},{19,3},{4,20},{20... | collective-permute-start | bytes 3145736 | tf_op jit(solution)/shard_map/ppermute | solution.py:230
  128.9 27.4 %collective-permute-start.18 = (bf16[256,2048]{1,0:T(8,128)(2,1)S(1)}, bf16[256,2048]{1,0:T(8,128)(2,1)}, u32[]{:S(2)}, u32[]{:S(2)}) collective-permute-start(bf16[256,2048]{1,0:T(8,128)(2,1)S(1)} %get-tuple-element.727.refs_0_), channel_id=1, source_target_pairs={{0,16},{16,0},{1,17},{17,1},{2,18},{18,2},{3,19},{19,3},{4,20},{20... | collective-permute-start | bytes 3145736 | tf_op jit(solution)/shard_map/ppermute | solution.py:230
  129.3 26.9 %collective-permute-start.21 = (bf16[256,2048]{1,0:T(8,128)(2,1)}, bf16[256,2048]{1,0:T(8,128)(2,1)}, u32[]{:S(2)}, u32[]{:S(2)}) collective-permute-start(bf16[256,2048]{1,0:T(8,128)(2,1)} %collective-permute-done.17.refs_3_), channel_id=1, source_target_pairs={{0,16},{16,0},{1,17},{17,1},{2,18},{18,2},{3,19},{19,3},{4,20},{20... | collective-permute-start | bytes 3145736 | tf_op jit(solution)/shard_map/ppermute | solution.py:230
  129.7 26.6 %collective-permute-start.19 = (bf16[256,2048]{1,0:T(8,128)(2,1)}, bf16[256,2048]{1,0:T(8,128)(2,1)}, u32[]{:S(2)}, u32[]{:S(2)}) collective-permute-start(bf16[256,2048]{1,0:T(8,128)(2,1)} %collective-permute-done.15.refs_1_), channel_id=1, source_target_pairs={{0,16},{16,0},{1,17},{17,1},{2,18},{18,2},{3,19},{19,3},{4,20},{20... | collective-permute-start | bytes 3145736 | tf_op jit(solution)/shard_map/ppermute | solution.py:230
  129.8 26.4 %collective-permute-start.20 = (bf16[256,2048]{1,0:T(8,128)(2,1)}, bf16[256,2048]{1,0:T(8,128)(2,1)}, u32[]{:S(2)}, u32[]{:S(2)}) collective-permute-start(bf16[256,2048]{1,0:T(8,128)(2,1)} %collective-permute-done.16.refs_2_), channel_id=1, source_target_pairs={{0,16},{16,0},{1,17},{17,1},{2,18},{18,2},{3,19},{19,3},{4,20},{20... | collective-permute-start | bytes 3145736 | tf_op jit(solution)/shard_map/ppermute | solution.py:230
  163.8 12.5 %all-to-all-start.9 = ((bf16[16,8,2048]{2,1,0:T(8,128)(2,1)}), bf16[16,8,2048]{2,1,0:T(8,128)(2,1)S(1)}, u32[]{:S(2)}, u32[]{:S(2)}) async-start(bf16[16,8,2048]{2,1,0:T(8,128)(2,1)} %bitcast.30), calls=%async_computation.9 | async-start | bytes 1048576 | tf_op jit(solution)/shard_map/all_to_all | solution.py:296
  513.9 49.8 %all-to-all-start.11 = ((bf16[8,2,1152]{2,1,0:T(2,128)(2,1)}), bf16[8,2,1152]{2,1,0:T(2,128)(2,1)S(1)}, u32[]{:S(2)}, u32[]{:S(2)}) async-start(bf16[8,2,1152]{2,1,0:T(2,128)(2,1)} %reshape.276), calls=%async_computation.11 | async-start | bytes 73728 | tf_op jit(solution)/shard_map/all_to_all | solution.py:324
  563.7 11.2 %all-to-all-start.10 = ((bf16[8,8,2048]{2,1,0:T(8,128)(2,1)}), bf16[8,8,2048]{2,1,0:T(8,128)(2,1)S(1)}, u32[]{:S(2)}, u32[]{:S(2)}) async-start(bf16[8,8,2048]{2,1,0:T(8,128)(2,1)} %get-tuple-element.221), calls=%async_computation.10 | async-start | bytes 524288 | tf_op jit(solution)/shard_map/all_to_all | solution.py:328
  (15 other events, 257.5 us)
